TPU v7x, 32 devices: a whole 2x2x4 slice. The times are simulated.
32 devices in a mesh: dp: 32 (over z, y, x, core).
Axes of the slice: x: 2, y: 2, z: 4, core: 2. Of those that a mesh axis runs over, the one named last changes fastest.
Arguments:
- img_emb: bfloat16 [16384, 1280], P('dp')
- txt_emb: bfloat16 [16384, 1280], P('dp')
- log_temp: float32 [], replicated
- logit_bias: float32 [], replicated
Outputs:
- output 1: float32 [], replicated
- output 2: float32 [16384, 1280], P('dp')
- output 3: float32 [16384, 1280], P('dp')
- output 4: float32 [], replicated
- output 5: float32 [], replicated
All inputs are finite; a program needn't handle non-finite values.
Results may differ from a plain program's by a relative error of at most 0.001.
Values are sent between devices in bfloat16 or wider.
A program may use at most 1 GiB of HBM per device.

v0:
```python
import jax
import jax.numpy as jnp
from jax import lax
from jax.sharding import PartitionSpec as P


def normalize_rows(emb):
    emb32 = emb.astype(jnp.float32)
    inv_norm = lax.rsqrt(jnp.sum(emb32 * emb32, axis=-1, keepdims=True))
    return emb32 * inv_norm, inv_norm


def project_back(unit_rows, inv_norm, grad_dir):
    radial = jnp.sum(unit_rows * grad_dir, axis=-1, keepdims=True)
    return (grad_dir - unit_rows * radial) * inv_norm


def pair_terms(img_b, txt_blk, temp_scale, logit_bias, label_signs):
    sim_vals = jnp.einsum('id,jd->ij', img_b, txt_blk, preferred_element_type=jnp.float32)
    logits = temp_scale * sim_vals + logit_bias
    weights = -label_signs * jax.nn.sigmoid(-label_signs * logits)
    weights_b = weights.astype(jnp.bfloat16)
    img_part = jnp.einsum('ij,jd->id', weights_b, txt_blk, preferred_element_type=jnp.float32)
    txt_part = jnp.einsum('ij,id->jd', weights_b, img_b, preferred_element_type=jnp.float32)
    stat_sums = jnp.stack([
        jnp.sum(jax.nn.softplus(-label_signs * logits)),
        jnp.sum(weights),
        jnp.sum(weights * sim_vals),
    ])
    return img_part, txt_part, stat_sums


def solution(mesh):
    group_size = mesh.shape['dp']
    shift_pairs = [(src_dev, (src_dev + 1) % group_size) for src_dev in range(group_size)]

    def local_fn(img_emb, txt_emb, log_temp, logit_bias):
        rows_dev = img_emb.shape[0]
        total_rows = rows_dev * group_size
        img_unit, img_inv = normalize_rows(img_emb)
        txt_unit, txt_inv = normalize_rows(txt_emb)
        img_b = img_unit.astype(jnp.bfloat16)
        txt_b = txt_unit.astype(jnp.bfloat16)
        temp_scale = jnp.exp(log_temp)
        local_ids = jnp.arange(rows_dev)
        diag_signs = jnp.where(local_ids[:, None] == local_ids[None, :], 1.0, -1.0)
        img_acc, txt_acc, stat_sums = pair_terms(img_b, txt_b, temp_scale, logit_bias, diag_signs)

        def visit_step(step_idx, loop_state):
            txt_blk, txt_acc, img_acc, stat_sums = loop_state
            txt_blk = lax.ppermute(txt_blk, 'dp', shift_pairs)
            txt_acc = lax.ppermute(txt_acc, 'dp', shift_pairs)
            img_part, txt_part, new_sums = pair_terms(img_b, txt_blk, temp_scale, logit_bias, -1.0)
            return txt_blk, txt_acc + txt_part, img_acc + img_part, stat_sums + new_sums

        loop_state = lax.fori_loop(0, group_size - 1, visit_step, (txt_b, txt_acc, img_acc, stat_sums))
        txt_acc = lax.ppermute(loop_state[1], 'dp', shift_pairs)
        img_acc = loop_state[2]
        stat_sums = lax.psum(loop_state[3], 'dp') / total_rows
        grad_img = project_back(img_unit, img_inv, temp_scale * img_acc)
        grad_txt = project_back(txt_unit, txt_inv, temp_scale * txt_acc)
        return stat_sums[0], grad_img, grad_txt, temp_scale * stat_sums[2], stat_sums[1]

    return jax.shard_map(
        local_fn,
        mesh=mesh,
        in_specs=(P('dp', None), P('dp', None), P(), P()),
        out_specs=(P(), P('dp', None), P('dp', None), P(), P()),
        check_vma=False,
    )
```

profile of v0, /device:TPU:0, one launch (start us, length us, event | category | flops | bytes accessed | tf_op | source)
XLA Modules:
  0.0 2009.3 jit_solution(9564211544149177506)
XLA Ops:
  15.5 1927.2 %while.16 = (s32[]{:T(128)}, bf16[512,1280]{1,0:T(8,128)(2,1)}, f32[512,1280]{1,0:T(8,128)}, f32[512,1280]{1,0:T(8,128)}, f32[3]{0:T(128)S(1)}, /*index=5*/f32[]...) while((s32[]{:T(128)}, bf16[512,1280]{1,0:T(8,128)(2,1)}, f32[512,1280]{1,0:T(8,128)}, ...), condition=%wide.region_9.10_spmd, body=%wide.region_5.9_spmd.sunk | while | flops 2021654528 | bytes 63439176 | solution.py:56
  78.7 48.7 %collective-permute-done = bf16[512,1280]{1,0:T(8,128)(2,1)S(1)} collective-permute-done((bf16[512,1280]{1,0:T(8,128)(2,1)}, bf16[512,1280]{1,0:T(8,128)(2,1)S(1)}, u32[]{:S(2)}, u32[]{:S(2)}) %collective-permute-start) | collective-permute-done | bytes 1310752 | tf_op jit(solution)/shard_map/while/body/eval_jaxpr/ppermute | solution.py:51
  140.8 48.7 %collective-permute-done = bf16[512,1280]{1,0:T(8,128)(2,1)S(1)} collective-permute-done((bf16[512,1280]{1,0:T(8,128)(2,1)}, bf16[512,1280]{1,0:T(8,128)(2,1)S(1)}, u32[]{:S(2)}, u32[]{:S(2)}) %collective-permute-start) | collective-permute-done | bytes 1310752 | tf_op jit(solution)/shard_map/while/body/eval_jaxpr/ppermute | solution.py:51
  265.1 48.7 %collective-permute-done = bf16[512,1280]{1,0:T(8,128)(2,1)S(1)} collective-permute-done((bf16[512,1280]{1,0:T(8,128)(2,1)}, bf16[512,1280]{1,0:T(8,128)(2,1)S(1)}, u32[]{:S(2)}, u32[]{:S(2)}) %collective-permute-start) | collective-permute-done | bytes 1310752 | tf_op jit(solution)/shard_map/while/body/eval_jaxpr/ppermute | solution.py:51
  327.2 48.7 %collective-permute-done = bf16[512,1280]{1,0:T(8,128)(2,1)S(1)} collective-permute-done((bf16[512,1280]{1,0:T(8,128)(2,1)}, bf16[512,1280]{1,0:T(8,128)(2,1)S(1)}, u32[]{:S(2)}, u32[]{:S(2)}) %collective-permute-start) | collective-permute-done | bytes 1310752 | tf_op jit(solution)/shard_map/while/body/eval_jaxpr/ppermute | solution.py:51
  451.5 48.7 %collective-permute-done = bf16[512,1280]{1,0:T(8,128)(2,1)S(1)} collective-permute-done((bf16[512,1280]{1,0:T(8,128)(2,1)}, bf16[512,1280]{1,0:T(8,128)(2,1)S(1)}, u32[]{:S(2)}, u32[]{:S(2)}) %collective-permute-start) | collective-permute-done | bytes 1310752 | tf_op jit(solution)/shard_map/while/body/eval_jaxpr/ppermute | solution.py:51
  513.6 48.7 %collective-permute-done = bf16[512,1280]{1,0:T(8,128)(2,1)S(1)} collective-permute-done((bf16[512,1280]{1,0:T(8,128)(2,1)}, bf16[512,1280]{1,0:T(8,128)(2,1)S(1)}, u32[]{:S(2)}, u32[]{:S(2)}) %collective-permute-start) | collective-permute-done | bytes 1310752 | tf_op jit(solution)/shard_map/while/body/eval_jaxpr/ppermute | solution.py:51
  637.9 48.7 %collective-permute-done = bf16[512,1280]{1,0:T(8,128)(2,1)S(1)} collective-permute-done((bf16[512,1280]{1,0:T(8,128)(2,1)}, bf16[512,1280]{1,0:T(8,128)(2,1)S(1)}, u32[]{:S(2)}, u32[]{:S(2)}) %collective-permute-start) | collective-permute-done | bytes 1310752 | tf_op jit(solution)/shard_map/while/body/eval_jaxpr/ppermute | solution.py:51
  700.0 48.7 %collective-permute-done = bf16[512,1280]{1,0:T(8,128)(2,1)S(1)} collective-permute-done((bf16[512,1280]{1,0:T(8,128)(2,1)}, bf16[512,1280]{1,0:T(8,128)(2,1)S(1)}, u32[]{:S(2)}, u32[]{:S(2)}) %collective-permute-start) | collective-permute-done | bytes 1310752 | tf_op jit(solution)/shard_map/while/body/eval_jaxpr/ppermute | solution.py:51
  762.1 48.7 %collective-permute-done = bf16[512,1280]{1,0:T(8,128)(2,1)S(1)} collective-permute-done((bf16[512,1280]{1,0:T(8,128)(2,1)}, bf16[512,1280]{1,0:T(8,128)(2,1)S(1)}, u32[]{:S(2)}, u32[]{:S(2)}) %collective-permute-start) | collective-permute-done | bytes 1310752 | tf_op jit(solution)/shard_map/while/body/eval_jaxpr/ppermute | solution.py:51
  824.3 48.7 %collective-permute-done = bf16[512,1280]{1,0:T(8,128)(2,1)S(1)} collective-permute-done((bf16[512,1280]{1,0:T(8,128)(2,1)}, bf16[512,1280]{1,0:T(8,128)(2,1)S(1)}, u32[]{:S(2)}, u32[]{:S(2)}) %collective-permute-start) | collective-permute-done | bytes 1310752 | tf_op jit(solution)/shard_map/while/body/eval_jaxpr/ppermute | solution.py:51
  886.4 48.7 %collective-permute-done = bf16[512,1280]{1,0:T(8,128)(2,1)S(1)} collective-permute-done((bf16[512,1280]{1,0:T(8,128)(2,1)}, bf16[512,1280]{1,0:T(8,128)(2,1)S(1)}, u32[]{:S(2)}, u32[]{:S(2)}) %collective-permute-start) | collective-permute-done | bytes 1310752 | tf_op jit(solution)/shard_map/while/body/eval_jaxpr/ppermute | solution.py:51
  948.5 48.7 %collective-permute-done = bf16[512,1280]{1,0:T(8,128)(2,1)S(1)} collective-permute-done((bf16[512,1280]{1,0:T(8,128)(2,1)}, bf16[512,1280]{1,0:T(8,128)(2,1)S(1)}, u32[]{:S(2)}, u32[]{:S(2)}) %collective-permute-start) | collective-permute-done | bytes 1310752 | tf_op jit(solution)/shard_map/while/body/eval_jaxpr/ppermute | solution.py:51
  1010.7 48.7 %collective-permute-done = bf16[512,1280]{1,0:T(8,128)(2,1)S(1)} collective-permute-done((bf16[512,1280]{1,0:T(8,128)(2,1)}, bf16[512,1280]{1,0:T(8,128)(2,1)S(1)}, u32[]{:S(2)}, u32[]{:S(2)}) %collective-permute-start) | collective-permute-done | bytes 1310752 | tf_op jit(solution)/shard_map/while/body/eval_jaxpr/ppermute | solution.py:51
  1072.8 48.7 %collective-permute-done = bf16[512,1280]{1,0:T(8,128)(2,1)S(1)} collective-permute-done((bf16[512,1280]{1,0:T(8,128)(2,1)}, bf16[512,1280]{1,0:T(8,128)(2,1)S(1)}, u32[]{:S(2)}, u32[]{:S(2)}) %collective-permute-start) | collective-permute-done | bytes 1310752 | tf_op jit(solution)/shard_map/while/body/eval_jaxpr/ppermute | solution.py:51
  1134.9 48.7 %collective-permute-done = bf16[512,1280]{1,0:T(8,128)(2,1)S(1)} collective-permute-done((bf16[512,1280]{1,0:T(8,128)(2,1)}, bf16[512,1280]{1,0:T(8,128)(2,1)S(1)}, u32[]{:S(2)}, u32[]{:S(2)}) %collective-permute-start) | collective-permute-done | bytes 1310752 | tf_op jit(solution)/shard_map/while/body/eval_jaxpr/ppermute | solution.py:51
  1259.2 48.7 %collective-permute-done = bf16[512,1280]{1,0:T(8,128)(2,1)S(1)} collective-permute-done((bf16[512,1280]{1,0:T(8,128)(2,1)}, bf16[512,1280]{1,0:T(8,128)(2,1)S(1)}, u32[]{:S(2)}, u32[]{:S(2)}) %collective-permute-start) | collective-permute-done | bytes 1310752 | tf_op jit(solution)/shard_map/while/body/eval_jaxpr/ppermute | solution.py:51
  1321.3 48.7 %collective-permute-done = bf16[512,1280]{1,0:T(8,128)(2,1)S(1)} collective-permute-done((bf16[512,1280]{1,0:T(8,128)(2,1)}, bf16[512,1280]{1,0:T(8,128)(2,1)S(1)}, u32[]{:S(2)}, u32[]{:S(2)}) %collective-permute-start) | collective-permute-done | bytes 1310752 | tf_op jit(solution)/shard_map/while/body/eval_jaxpr/ppermute | solution.py:51
  1445.6 48.7 %collective-permute-done = bf16[512,1280]{1,0:T(8,128)(2,1)S(1)} collective-permute-done((bf16[512,1280]{1,0:T(8,128)(2,1)}, bf16[512,1280]{1,0:T(8,128)(2,1)S(1)}, u32[]{:S(2)}, u32[]{:S(2)}) %collective-permute-start) | collective-permute-done | bytes 1310752 | tf_op jit(solution)/shard_map/while/body/eval_jaxpr/ppermute | solution.py:51
  1507.7 48.7 %collective-permute-done = bf16[512,1280]{1,0:T(8,128)(2,1)S(1)} collective-permute-done((bf16[512,1280]{1,0:T(8,128)(2,1)}, bf16[512,1280]{1,0:T(8,128)(2,1)S(1)}, u32[]{:S(2)}, u32[]{:S(2)}) %collective-permute-start) | collective-permute-done | bytes 1310752 | tf_op jit(solution)/shard_map/while/body/eval_jaxpr/ppermute | solution.py:51
  1632.0 48.7 %collective-permute-done = bf16[512,1280]{1,0:T(8,128)(2,1)S(1)} collective-permute-done((bf16[512,1280]{1,0:T(8,128)(2,1)}, bf16[512,1280]{1,0:T(8,128)(2,1)S(1)}, u32[]{:S(2)}, u32[]{:S(2)}) %collective-permute-start) | collective-permute-done | bytes 1310752 | tf_op jit(solution)/shard_map/while/body/eval_jaxpr/ppermute | solution.py:51
  1694.1 48.7 %collective-permute-done = bf16[512,1280]{1,0:T(8,128)(2,1)S(1)} collective-permute-done((bf16[512,1280]{1,0:T(8,128)(2,1)}, bf16[512,1280]{1,0:T(8,128)(2,1)S(1)}, u32[]{:S(2)}, u32[]{:S(2)}) %collective-permute-start) | collective-permute-done | bytes 1310752 | tf_op jit(solution)/shard_map/while/body/eval_jaxpr/ppermute | solution.py:51
  1880.5 48.8 %collective-permute-done = bf16[512,1280]{1,0:T(8,128)(2,1)S(1)} collective-permute-done((bf16[512,1280]{1,0:T(8,128)(2,1)}, bf16[512,1280]{1,0:T(8,128)(2,1)S(1)}, u32[]{:S(2)}, u32[]{:S(2)}) %collective-permute-start) | collective-permute-done | bytes 1310752 | tf_op jit(solution)/shard_map/while/body/eval_jaxpr/ppermute | solution.py:51
  1942.7 53.5 %psum.7 = f32[3]{0:T(128)S(1)} all-reduce(f32[3]{0:T(128)S(1)} %get-tuple-element.49), channel_id=1, replica_groups=mesh['dp'=32] {'dp'}, use_global_device_ids=true, to_apply=%region_10.11 | all-reduce | flops 3 | bytes 24 | tf_op jit(solution)/shard_map/psum | solution.py:59
  (472 shorter events, 879.1 us)
Async XLA Ops:
  15.5 58.2 %collective-permute-start.1 = (f32[512,1280]{1,0:T(8,128)}, f32[512,1280]{1,0:T(8,128)}, u32[]{:S(2)}, u32[]{:S(2)}) collective-permute-start(f32[512,1280]{1,0:T(8,128)} %get-tuple-element.149), channel_id=1, source_target_pairs={{0,1},{1,2},{2,3},{3,4},{4,5},{5,6},{6,7},{7,8},{8,9},{9,10},{10,1... | collective-permute-start | bytes 7864328 | tf_op jit(solution)/shard_map/while/body/eval_jaxpr/ppermute | solution.py:52
  78.7 57.1 %collective-permute-start.1 = (f32[512,1280]{1,0:T(8,128)}, f32[512,1280]{1,0:T(8,128)}, u32[]{:S(2)}, u32[]{:S(2)}) collective-permute-start(f32[512,1280]{1,0:T(8,128)} %get-tuple-element.149), channel_id=1, source_target_pairs={{0,1},{1,2},{2,3},{3,4},{4,5},{5,6},{6,7},{7,8},{8,9},{9,10},{10,1... | collective-permute-start | bytes 7864328 | tf_op jit(solution)/shard_map/while/body/eval_jaxpr/ppermute | solution.py:52
  140.8 57.1 %collective-permute-start.1 = (f32[512,1280]{1,0:T(8,128)}, f32[512,1280]{1,0:T(8,128)}, u32[]{:S(2)}, u32[]{:S(2)}) collective-permute-start(f32[512,1280]{1,0:T(8,128)} %get-tuple-element.149), channel_id=1, source_target_pairs={{0,1},{1,2},{2,3},{3,4},{4,5},{5,6},{6,7},{7,8},{8,9},{9,10},{10,1... | collective-permute-start | bytes 7864328 | tf_op jit(solution)/shard_map/while/body/eval_jaxpr/ppermute | solution.py:52
  203.0 57.1 %collective-permute-start.1 = (f32[512,1280]{1,0:T(8,128)}, f32[512,1280]{1,0:T(8,128)}, u32[]{:S(2)}, u32[]{:S(2)}) collective-permute-start(f32[512,1280]{1,0:T(8,128)} %get-tuple-element.149), channel_id=1, source_target_pairs={{0,1},{1,2},{2,3},{3,4},{4,5},{5,6},{6,7},{7,8},{8,9},{9,10},{10,1... | collective-permute-start | bytes 7864328 | tf_op jit(solution)/shard_map/while/body/eval_jaxpr/ppermute | solution.py:52
  265.1 57.1 %collective-permute-start.1 = (f32[512,1280]{1,0:T(8,128)}, f32[512,1280]{1,0:T(8,128)}, u32[]{:S(2)}, u32[]{:S(2)}) collective-permute-start(f32[512,1280]{1,0:T(8,128)} %get-tuple-element.149), channel_id=1, source_target_pairs={{0,1},{1,2},{2,3},{3,4},{4,5},{5,6},{6,7},{7,8},{8,9},{9,10},{10,1... | collective-permute-start | bytes 7864328 | tf_op jit(solution)/shard_map/while/body/eval_jaxpr/ppermute | solution.py:52
  327.2 57.1 %collective-permute-start.1 = (f32[512,1280]{1,0:T(8,128)}, f32[512,1280]{1,0:T(8,128)}, u32[]{:S(2)}, u32[]{:S(2)}) collective-permute-start(f32[512,1280]{1,0:T(8,128)} %get-tuple-element.149), channel_id=1, source_target_pairs={{0,1},{1,2},{2,3},{3,4},{4,5},{5,6},{6,7},{7,8},{8,9},{9,10},{10,1... | collective-permute-start | bytes 7864328 | tf_op jit(solution)/shard_map/while/body/eval_jaxpr/ppermute | solution.py:52
  451.5 57.1 %collective-permute-start.1 = (f32[512,1280]{1,0:T(8,128)}, f32[512,1280]{1,0:T(8,128)}, u32[]{:S(2)}, u32[]{:S(2)}) collective-permute-start(f32[512,1280]{1,0:T(8,128)} %get-tuple-element.149), channel_id=1, source_target_pairs={{0,1},{1,2},{2,3},{3,4},{4,5},{5,6},{6,7},{7,8},{8,9},{9,10},{10,1... | collective-permute-start | bytes 7864328 | tf_op jit(solution)/shard_map/while/body/eval_jaxpr/ppermute | solution.py:52
  513.6 57.1 %collective-permute-start.1 = (f32[512,1280]{1,0:T(8,128)}, f32[512,1280]{1,0:T(8,128)}, u32[]{:S(2)}, u32[]{:S(2)}) collective-permute-start(f32[512,1280]{1,0:T(8,128)} %get-tuple-element.149), channel_id=1, source_target_pairs={{0,1},{1,2},{2,3},{3,4},{4,5},{5,6},{6,7},{7,8},{8,9},{9,10},{10,1... | collective-permute-start | bytes 7864328 | tf_op jit(solution)/shard_map/while/body/eval_jaxpr/ppermute | solution.py:52
  637.9 57.1 %collective-permute-start.1 = (f32[512,1280]{1,0:T(8,128)}, f32[512,1280]{1,0:T(8,128)}, u32[]{:S(2)}, u32[]{:S(2)}) collective-permute-start(f32[512,1280]{1,0:T(8,128)} %get-tuple-element.149), channel_id=1, source_target_pairs={{0,1},{1,2},{2,3},{3,4},{4,5},{5,6},{6,7},{7,8},{8,9},{9,10},{10,1... | collective-permute-start | bytes 7864328 | tf_op jit(solution)/shard_map/while/body/eval_jaxpr/ppermute | solution.py:52
  700.0 57.1 %collective-permute-start.1 = (f32[512,1280]{1,0:T(8,128)}, f32[512,1280]{1,0:T(8,128)}, u32[]{:S(2)}, u32[]{:S(2)}) collective-permute-start(f32[512,1280]{1,0:T(8,128)} %get-tuple-element.149), channel_id=1, source_target_pairs={{0,1},{1,2},{2,3},{3,4},{4,5},{5,6},{6,7},{7,8},{8,9},{9,10},{10,1... | collective-permute-start | bytes 7864328 | tf_op jit(solution)/shard_map/while/body/eval_jaxpr/ppermute | solution.py:52
  824.3 57.1 %collective-permute-start.1 = (f32[512,1280]{1,0:T(8,128)}, f32[512,1280]{1,0:T(8,128)}, u32[]{:S(2)}, u32[]{:S(2)}) collective-permute-start(f32[512,1280]{1,0:T(8,128)} %get-tuple-element.149), channel_id=1, source_target_pairs={{0,1},{1,2},{2,3},{3,4},{4,5},{5,6},{6,7},{7,8},{8,9},{9,10},{10,1... | collective-permute-start | bytes 7864328 | tf_op jit(solution)/shard_map/while/body/eval_jaxpr/ppermute | solution.py:52
  886.4 57.1 %collective-permute-start.1 = (f32[512,1280]{1,0:T(8,128)}, f32[512,1280]{1,0:T(8,128)}, u32[]{:S(2)}, u32[]{:S(2)}) collective-permute-start(f32[512,1280]{1,0:T(8,128)} %get-tuple-element.149), channel_id=1, source_target_pairs={{0,1},{1,2},{2,3},{3,4},{4,5},{5,6},{6,7},{7,8},{8,9},{9,10},{10,1... | collective-permute-start | bytes 7864328 | tf_op jit(solution)/shard_map/while/body/eval_jaxpr/ppermute | solution.py:52
  948.5 57.1 %collective-permute-start.1 = (f32[512,1280]{1,0:T(8,128)}, f32[512,1280]{1,0:T(8,128)}, u32[]{:S(2)}, u32[]{:S(2)}) collective-permute-start(f32[512,1280]{1,0:T(8,128)} %get-tuple-element.149), channel_id=1, source_target_pairs={{0,1},{1,2},{2,3},{3,4},{4,5},{5,6},{6,7},{7,8},{8,9},{9,10},{10,1... | collective-permute-start | bytes 7864328 | tf_op jit(solution)/shard_map/while/body/eval_jaxpr/ppermute | solution.py:52
  1072.8 57.1 %collective-permute-start.1 = (f32[512,1280]{1,0:T(8,128)}, f32[512,1280]{1,0:T(8,128)}, u32[]{:S(2)}, u32[]{:S(2)}) collective-permute-start(f32[512,1280]{1,0:T(8,128)} %get-tuple-element.149), channel_id=1, source_target_pairs={{0,1},{1,2},{2,3},{3,4},{4,5},{5,6},{6,7},{7,8},{8,9},{9,10},{10,1... | collective-permute-start | bytes 7864328 | tf_op jit(solution)/shard_map/while/body/eval_jaxpr/ppermute | solution.py:52
  1134.9 57.1 %collective-permute-start.1 = (f32[512,1280]{1,0:T(8,128)}, f32[512,1280]{1,0:T(8,128)}, u32[]{:S(2)}, u32[]{:S(2)}) collective-permute-start(f32[512,1280]{1,0:T(8,128)} %get-tuple-element.149), channel_id=1, source_target_pairs={{0,1},{1,2},{2,3},{3,4},{4,5},{5,6},{6,7},{7,8},{8,9},{9,10},{10,1... | collective-permute-start | bytes 7864328 | tf_op jit(solution)/shard_map/while/body/eval_jaxpr/ppermute | solution.py:52
  1259.2 57.1 %collective-permute-start.1 = (f32[512,1280]{1,0:T(8,128)}, f32[512,1280]{1,0:T(8,128)}, u32[]{:S(2)}, u32[]{:S(2)}) collective-permute-start(f32[512,1280]{1,0:T(8,128)} %get-tuple-element.149), channel_id=1, source_target_pairs={{0,1},{1,2},{2,3},{3,4},{4,5},{5,6},{6,7},{7,8},{8,9},{9,10},{10,1... | collective-permute-start | bytes 7864328 | tf_op jit(solution)/shard_map/while/body/eval_jaxpr/ppermute | solution.py:52
  1321.3 57.1 %collective-permute-start.1 = (f32[512,1280]{1,0:T(8,128)}, f32[512,1280]{1,0:T(8,128)}, u32[]{:S(2)}, u32[]{:S(2)}) collective-permute-start(f32[512,1280]{1,0:T(8,128)} %get-tuple-element.149), channel_id=1, source_target_pairs={{0,1},{1,2},{2,3},{3,4},{4,5},{5,6},{6,7},{7,8},{8,9},{9,10},{10,1... | collective-permute-start | bytes 7864328 | tf_op jit(solution)/shard_map/while/body/eval_jaxpr/ppermute | solution.py:52
  1445.6 57.1 %collective-permute-start.1 = (f32[512,1280]{1,0:T(8,128)}, f32[512,1280]{1,0:T(8,128)}, u32[]{:S(2)}, u32[]{:S(2)}) collective-permute-start(f32[512,1280]{1,0:T(8,128)} %get-tuple-element.149), channel_id=1, source_target_pairs={{0,1},{1,2},{2,3},{3,4},{4,5},{5,6},{6,7},{7,8},{8,9},{9,10},{10,1... | collective-permute-start | bytes 7864328 | tf_op jit(solution)/shard_map/while/body/eval_jaxpr/ppermute | solution.py:52
  1507.7 57.1 %collective-permute-start.1 = (f32[512,1280]{1,0:T(8,128)}, f32[512,1280]{1,0:T(8,128)}, u32[]{:S(2)}, u32[]{:S(2)}) collective-permute-start(f32[512,1280]{1,0:T(8,128)} %get-tuple-element.149), channel_id=1, source_target_pairs={{0,1},{1,2},{2,3},{3,4},{4,5},{5,6},{6,7},{7,8},{8,9},{9,10},{10,1... | collective-permute-start | bytes 7864328 | tf_op jit(solution)/shard_map/while/body/eval_jaxpr/ppermute | solution.py:52
  1632.0 57.1 %collective-permute-start.1 = (f32[512,1280]{1,0:T(8,128)}, f32[512,1280]{1,0:T(8,128)}, u32[]{:S(2)}, u32[]{:S(2)}) collective-permute-start(f32[512,1280]{1,0:T(8,128)} %get-tuple-element.149), channel_id=1, source_target_pairs={{0,1},{1,2},{2,3},{3,4},{4,5},{5,6},{6,7},{7,8},{8,9},{9,10},{10,1... | collective-permute-start | bytes 7864328 | tf_op jit(solution)/shard_map/while/body/eval_jaxpr/ppermute | solution.py:52
  1694.1 57.1 %collective-permute-start.1 = (f32[512,1280]{1,0:T(8,128)}, f32[512,1280]{1,0:T(8,128)}, u32[]{:S(2)}, u32[]{:S(2)}) collective-permute-start(f32[512,1280]{1,0:T(8,128)} %get-tuple-element.149), channel_id=1, source_target_pairs={{0,1},{1,2},{2,3},{3,4},{4,5},{5,6},{6,7},{7,8},{8,9},{9,10},{10,1... | collective-permute-start | bytes 7864328 | tf_op jit(solution)/shard_map/while/body/eval_jaxpr/ppermute | solution.py:52
  1818.3 57.1 %collective-permute-start.1 = (f32[512,1280]{1,0:T(8,128)}, f32[512,1280]{1,0:T(8,128)}, u32[]{:S(2)}, u32[]{:S(2)}) collective-permute-start(f32[512,1280]{1,0:T(8,128)} %get-tuple-element.149), channel_id=1, source_target_pairs={{0,1},{1,2},{2,3},{3,4},{4,5},{5,6},{6,7},{7,8},{8,9},{9,10},{10,1... | collective-permute-start | bytes 7864328 | tf_op jit(solution)/shard_map/while/body/eval_jaxpr/ppermute | solution.py:52
  1880.5 57.2 %collective-permute-start.1 = (f32[512,1280]{1,0:T(8,128)}, f32[512,1280]{1,0:T(8,128)}, u32[]{:S(2)}, u32[]{:S(2)}) collective-permute-start(f32[512,1280]{1,0:T(8,128)} %get-tuple-element.149), channel_id=1, source_target_pairs={{0,1},{1,2},{2,3},{3,4},{4,5},{5,6},{6,7},{7,8},{8,9},{9,10},{10,1... | collective-permute-start | bytes 7864328 | tf_op jit(solution)/shard_map/while/body/eval_jaxpr/ppermute | solution.py:52
  1942.7 59.4 %collective-permute-start.2 = (f32[512,1280]{1,0:T(8,128)}, f32[512,1280]{1,0:T(8,128)}, u32[]{:S(2)}, u32[]{:S(2)}) collective-permute-start(f32[512,1280]{1,0:T(8,128)} %get-tuple-element.51), channel_id=1, source_target_pairs={{0,1},{1,2},{2,3},{3,4},{4,5},{5,6},{6,7},{7,8},{8,9},{9,10},{10,1... | collective-permute-start | bytes 7864328 | tf_op jit(solution)/shard_map/ppermute | solution.py:57
  (138 other events, 3848.7 us)
where the time goes:
time: 2010 us
  waiting for transfers between devices  1510 us (75%)
  matrix products  326 us (16%)
  other arithmetic  78.7 us (4%)
  blocking collectives  53.5 us (3%)
  local copies, waits for them, and re-layouts  34.8 us (2%)
    ppermute x31, waiting for transfers between devices, visit_step(): txt_blk = lax.ppermute(txt_blk, 'dp', shift_pairs)  1510 us
    dot_general x32, matrix products, pair_terms(): jnp.einsum('ij,id->jd', weights_b, img_b, preferred_element_type=jnp.floa...  159 us
    dot_general x32, matrix products, pair_terms(): jnp.einsum('id,jd->ij', img_b, txt_blk, preferred_element_type=jnp.float32)  100 us
    dot_general x32, matrix products, pair_terms(): jnp.einsum('ij,jd->id', weights_b, txt_blk, preferred_element_type=jnp.fl...  66.2 us
    add x31, other arithmetic, visit_step(): stat_sums + new_sums  62.3 us
    psum x1, blocking collectives, local_fn(): stat_sums = lax.psum(loop_state[3], 'dp') / total_rows  53.5 us
  transfers between devices with their start and end apart: 63, of which 31 were waited for; matrix products, arithmetic and copies ran while one was open for 13% of the time, Pallas kernels for 0%

commit v1 on v0

v1 whole, which is shorter than its diff:
```python
import jax
import jax.numpy as jnp
from jax import lax
from jax.sharding import PartitionSpec as P


def normalize_rows(emb):
    emb32 = emb.astype(jnp.float32)
    inv_norm = lax.rsqrt(jnp.sum(emb32 * emb32, axis=-1, keepdims=True))
    return emb32 * inv_norm, inv_norm


def project_back(unit_rows, inv_norm, grad_dir):
    radial = jnp.sum(unit_rows * grad_dir, axis=-1, keepdims=True)
    return (grad_dir - unit_rows * radial) * inv_norm


def solution(mesh):
    n_dev = mesh.shape['dp']
    plane = 8
    n_z = n_dev // plane
    col_groups = [[b + plane * z for z in range(n_z)] for b in range(plane)]
    row_groups = [[z * plane + b for b in range(plane)] for z in range(n_z)]

    def local_fn(img_emb, txt_emb, log_temp, logit_bias):
        rows = img_emb.shape[0]
        total_rows = rows * n_dev
        me = lax.axis_index('dp')
        img_unit, img_inv = normalize_rows(img_emb)
        txt_unit, txt_inv = normalize_rows(txt_emb)
        temp_scale = jnp.exp(log_temp)
        xs = lax.all_gather(img_unit.astype(jnp.bfloat16), 'dp', axis_index_groups=col_groups, tiled=True)
        ys = lax.all_gather(txt_unit.astype(jnp.bfloat16), 'dp', axis_index_groups=row_groups, tiled=True)
        i = jnp.arange(xs.shape[0])
        j = jnp.arange(ys.shape[0])
        gi = (i // rows * plane + me % plane) * rows + i % rows
        gj = (me // plane) * plane * rows + j
        sim = jnp.einsum('id,jd->ij', xs, ys, preferred_element_type=jnp.float32)
        logits = temp_scale * sim + logit_bias
        sign = jnp.where(gi[:, None] == gj[None, :], 1.0, -1.0)
        weights = -sign * jax.nn.sigmoid(-sign * logits)
        wb = weights.astype(jnp.bfloat16)
        u = jnp.einsum('ij,jd->id', wb, ys, preferred_element_type=jnp.float32)
        v = jnp.einsum('ij,id->jd', wb, xs, preferred_element_type=jnp.float32)
        stats = jnp.stack([jnp.sum(jax.nn.softplus(-sign * logits)), jnp.sum(weights), jnp.sum(weights * sim)])
        u = lax.psum_scatter(u, 'dp', scatter_dimension=0, axis_index_groups=col_groups, tiled=True)
        v = lax.psum_scatter(v, 'dp', scatter_dimension=0, axis_index_groups=row_groups, tiled=True)
        stats = lax.psum(stats, 'dp') / total_rows
        grad_img = project_back(img_unit, img_inv, temp_scale * u)
        grad_txt = project_back(txt_unit, txt_inv, temp_scale * v)
        return stats[0], grad_img, grad_txt, temp_scale * stats[2], stats[1]

    return jax.shard_map(
        local_fn,
        mesh=mesh,
        in_specs=(P('dp', None), P('dp', None), P(), P()),
        out_specs=(P(), P('dp', None), P('dp', None), P(), P()),
        check_vma=False,
    )
```

time: 2010 us -> 595 us (0.30)
  waiting for transfers between devices: 1510 us -> 400 us
  matrix products: 326 us -> 116 us
  other arithmetic: 78.7 us -> 17.2 us
  local copies, waits for them, and re-layouts: 34.8 us -> 1.84 us
    ppermute x63 -> x0, waiting for transfers between devices: 1510 us -> none  [the longest x31 1510 us: visit_step(): txt_blk = lax.ppermute(txt_blk, 'dp', shift_pairs)]
    reduce_scatter x0 -> x2, waiting for transfers between devices: none -> 239 us  [the longest x1 135 us: local_fn(): lax.psum_scatter(v, 'dp', scatter_dimension=0, axis_index_groups=row_grou...]
    dot_general x96 -> x3, matrix products: 326 us -> 116 us  [the longest x1 57.5 us: local_fn(): sim = jnp.einsum('id,jd->ij', xs, ys, preferred_element_type=jnp.float32)]
    all_gather x0 -> x2, waiting for transfers between devices: none -> 161 us  [the longest x1 96.7 us: local_fn(): lax.all_gather(img_unit.astype(jnp.bfloat16), 'dp', axis_index_groups=col...]
    add x31 -> x2, other arithmetic: 62.3 us -> 0.02 us  [the longest x1 0.01 us: local_fn(): gi = (i // rows * plane + me % plane) * rows + i % rows]
    while x217 -> x0, local copies, waits for them, and re-layouts: 34.1 us -> none
  transfers between devices with their start and end apart: 63 -> 4, of which waited for: 31 -> 4; matrix products, arithmetic and copies ran while one was open for 13% -> 6% of each run, Pallas kernels for 0% -> 0%
where the time goes in v1:
time: 595 us; the launch traced here: 594 us
  waiting for transfers between devices  400 us (67%)
  matrix products  116 us (19%)
  blocking collectives  42.5 us (7%)
  other arithmetic  17.2 us (3%)
  between operations  17 us (3%)
    reduce_scatter x1, waiting for transfers between devices, local_fn(): lax.psum_scatter(v, 'dp', scatter_dimension=0, axis_index_groups=row_grou...  135 us
    reduce_scatter x1, waiting for transfers between devices, local_fn(): lax.psum_scatter(u, 'dp', scatter_dimension=0, axis_index_groups=col_grou...  104 us
    all_gather x1, waiting for transfers between devices, local_fn(): lax.all_gather(img_unit.astype(jnp.bfloat16), 'dp', axis_index_groups=col...  96.7 us
    all_gather x1, waiting for transfers between devices, local_fn(): lax.all_gather(txt_unit.astype(jnp.bfloat16), 'dp', axis_index_groups=row...  64.1 us
    dot_general x1, matrix products, local_fn(): sim = jnp.einsum('id,jd->ij', xs, ys, preferred_element_type=jnp.float32)  57.5 us
    psum x1, blocking collectives, local_fn(): stats = lax.psum(stats, 'dp') / total_rows  42.5 us
    dot_general x1, matrix products, local_fn(): u = jnp.einsum('ij,jd->id', wb, ys, preferred_element_type=jnp.float32)  29.1 us
    dot_general x1, matrix products, local_fn(): v = jnp.einsum('ij,id->jd', wb, xs, preferred_element_type=jnp.float32)  29 us
  transfers between devices with their start and end apart: 4, of which 4 were waited for; matrix products, arithmetic and copies ran while one was open for 6% of the time, Pallas kernels for 0%

profile of v1, /device:TPU:0, one launch (start us, length us, event | category | flops | bytes accessed | tf_op | source)
XLA Modules:
  0.0 594.3 jit_solution(8710679026870964538)
XLA Ops:
  7.2 1.7 fusion.14
  9.0 0.5 copy-done.5
  9.5 2.7 fusion.10
  12.3 0.3 fusion.18
  12.6 0.5 copy-done.7
  13.1 1.3 fusion.7
  14.5 0.0 reduce-scatter.3.cloned.1.call-start
  15.9 96.7 %all-gather.3.cloned.1.call-done = bf16[2048,1280]{1,0:T(8,128)(2,1)} async-done(((bf16[512,1280]{1,0:T(8,128)(2,1)}), bf16[2048,1280]{1,0:T(8,128)(2,1)}) %all-gather.3.cloned.1.call-update) | async-done | bytes 5242896 | tf_op jit(solution)/shard_map/all_gather | solution.py:32
  112.6 64.1 %all-gather.5.cloned.1.call-done = bf16[4096,1280]{1,0:T(8,128)(2,1)} async-done(((bf16[512,1280]{1,0:T(8,128)(2,1)}), bf16[4096,1280]{1,0:T(8,128)(2,1)}) %all-gather.5.cloned.1.call-update) | async-done | bytes 10485776 | tf_op jit(solution)/shard_map/all_gather | solution.py:33
  176.7 57.5 %fusion = (f32[]{:T(128)}, f32[]{:T(128)}, f32[]{:T(128)}, bf16[2048,4096]{1,0:T(8,128)(2,1)}) fusion(f32[]{:T(128)S(6)} %copy.10, f32[]{:T(128)S(6)} %exp.10, s32[4096]{0:T(1024)S(1)} %iota_add_fusion, s32[2048]{0:T(1024)S(1)} %fusion.28, bf16[2048,1280]{1,0:T(8,128)(2,1)} %all-gather.3.cloned.1.call-done, bf16[4096,1280]{1,0:T(8,128)(2,1)} %all-gather.5.cloned.1.call-done), kind=kOutput, calls=%fused_computation.1 | convolution fusion | flops 21650997248 | bytes 32530452 | tf_op jit(solution)/shard_map/id,jd->ij/dot_general | solution.py:38
  234.2 29.1 %fusion.3 = f32[2048,1280]{1,0:T(8,128)} fusion(bf16[4096,1280]{1,0:T(8,128)(2,1)} %all-gather.5.cloned.1.call-done, bf16[2048,4096]{1,0:T(8,128)(2,1)} %get-tuple-element.8), kind=kOutput, calls=%fused_computation.8 | convolution fusion | flops 21474836480 | bytes 37748736 | tf_op jit(solution)/shard_map/ij,jd->id/dot_general | solution.py:43
  263.4 0.0 reduce-scatter.5.cloned.1.call-start
  263.4 29.0 %fusion.1 = f32[4096,1280]{1,0:T(8,128)} fusion(bf16[2048,1280]{1,0:T(8,128)(2,1)} %all-gather.3.cloned.1.call-done, bf16[2048,4096]{1,0:T(8,128)(2,1)} %get-tuple-element.8), kind=kOutput, calls=%fused_computation.6 | convolution fusion | flops 21474836480 | bytes 42991616 | tf_op jit(solution)/shard_map/ij,id->jd/dot_general | solution.py:44
  292.4 2.1 pad_maximum_fusion
  294.5 42.5 %psum.7 = f32[3]{0:T(128)S(1)} all-reduce(f32[3]{0:T(128)S(1)} %pad_maximum_fusion), channel_id=1, replica_groups=mesh['dp'=32] {'dp'}, use_global_device_ids=true, to_apply=%region_5.6 | all-reduce | flops 3 | bytes 24 | tf_op jit(solution)/shard_map/psum | solution.py:48
  337.0 0.6 fusion.30
  338.3 104.2 %reduce-scatter.3.cloned.1.call-done = f32[512,1280]{1,0:T(8,128)} async-done(((f32[2048,1280]{1,0:T(8,128)}), f32[512,1280]{1,0:T(8,128)}) %reduce-scatter.3.cloned.1.call-update) | async-done | bytes 2621456 | tf_op jit(solution)/shard_map/reduce_scatter | solution.py:46
  442.5 2.4 fusion.11
  445.0 0.1 copy-done.3
  445.0 2.1 fusion.13
  447.1 134.9 %reduce-scatter.5.cloned.1.call-done = f32[512,1280]{1,0:T(8,128)} async-done(((f32[4096,1280]{1,0:T(8,128)}), f32[512,1280]{1,0:T(8,128)}) %reduce-scatter.5.cloned.1.call-update) | async-done | bytes 2621456 | tf_op jit(solution)/shard_map/reduce_scatter | solution.py:47
  582.0 2.5 fusion.15
  584.5 0.1 copy-done.4
  584.6 2.1 fusion.17
  (25 shorter events, 0.2 us)
Async XLA Ops:
  7.2 5.1 copy-start.1
  7.2 105.5 %all-gather.3.cloned.1.call-start = ((), (), s32[]{:S(2)}) async-start(), calls=%async_computation.2 | async-start | bytes 6553600 | tf_op jit(solution)/shard_map/all_gather | solution.py:32
  9.0 0.5 copy-start.5
  12.2 164.5 %all-gather.5.cloned.1.call-start = ((), (), s32[]{:S(2)}) async-start(), calls=%async_computation.3 | async-start | bytes 11796480 | tf_op jit(solution)/shard_map/all_gather | solution.py:33
  12.6 0.5 copy-start.7
  14.5 428.0 %reduce-scatter.3.cloned.1.call-start = ((), (), s32[]{:S(2)}) async-start(), calls=%async_computation.4 | async-start | bytes 13107200 | tf_op jit(solution)/shard_map/reduce_scatter | solution.py:46
  263.4 318.7 %reduce-scatter.5.cloned.1.call-start = ((), (), s32[]{:S(2)}) async-start(), calls=%async_computation.5 | async-start | bytes 23592960 | tf_op jit(solution)/shard_map/reduce_scatter | solution.py:47
  292.4 150.1 %copy-start = (bf16[512,1280]{1,0:T(8,128)(2,1)S(1)}, bf16[512,1280]{1,0:T(8,128)(2,1)}, u32[]{:S(2)}) copy-start(bf16[512,1280]{1,0:T(8,128)(2,1)} %param.4) | copy-start | bytes 3932164
  292.4 150.1 %copy-start.6 = (f32[512]{0:T(512)S(1)}, f32[512]{0:T(512)}, u32[]{:S(2)}) copy-start(f32[512]{0:T(512)} %copy-done.5) | copy-start | bytes 6148
  442.5 2.5 copy-start.3
  445.0 137.0 %copy-start.2 = (bf16[512,1280]{1,0:T(8,128)(2,1)S(1)}, bf16[512,1280]{1,0:T(8,128)(2,1)}, u32[]{:S(2)}) copy-start(bf16[512,1280]{1,0:T(8,128)(2,1)} %param.5) | copy-start | bytes 3932164
  445.0 137.0 %copy-start.8 = (f32[512]{0:T(512)S(1)}, f32[512]{0:T(512)}, u32[]{:S(2)}) copy-start(f32[512]{0:T(512)} %copy-done.7) | copy-start | bytes 6148
  582.0 2.5 copy-start.4
Sparse Core Ops, SparseCore 0:
  12.3 100.2 all-gather.2
  115.1 61.5 all-gather.4
  263.5 178.9 reduce-scatter.2
  446.0 135.9 reduce-scatter.4

commit v2 on v1

v2 whole, which is shorter than its diff:
```python
import functools
import math

import jax
import jax.numpy as jnp
from jax import lax
from jax.experimental import pallas as pl
from jax.experimental.pallas import tpu as pltpu
from jax.sharding import PartitionSpec as P

F32 = jnp.float32
BF16 = jnp.bfloat16
MESH = pl.DeviceIdType.MESH
LOG2E = math.log2(math.e)
LN2 = math.log(2.0)
PLANE = 8
RING = 4
PIECES = 2


def dot_f32(lhs, rhs, lhs_dim, rhs_dim):
    return lax.dot_general(lhs, rhs, (((lhs_dim,), (rhs_dim,)), ((), ())), preferred_element_type=F32)


def pick(table, idx):
    out = jnp.int32(table[0])
    for pos in range(1, len(table)):
        out = jnp.where(idx == pos, jnp.int32(table[pos]), out)
    return out


def loss_kernel(scal, img_hbm, txt_hbm, u_out, v_out, stat_out,
                X, Y, H, PU, RU, DV, WV, RV, ST, SE,
                ld_sem, gx_s, gx_r, gy_s, gy_r, yd_s, yd_r, ru_s, ru_r, rv_s, rv_r,
                dv_s, dv_r, se_s, se_r, out_sem, credit):
    rows, width = img_hbm.shape
    half = rows // 2
    piece = half // PIECES
    me = lax.axis_index('dp')
    z = me // PLANE
    rem = me % PLANE
    y = rem // 4
    x = (rem // 2) % 2
    core = rem % 2
    q = 2 * y + (x + y - 2 * x * y)

    def z_dev(step):
        return ((z + step) % RING) * PLANE + rem

    def q_dev(step):
        q2 = (q + step) % RING
        y2 = q2 // 2
        b2 = q2 % 2
        x2 = b2 + y2 - 2 * b2 * y2
        return z * PLANE + y2 * 4 + x2 * 2 + core

    partner = me + 1 - 2 * core
    z_peers = [z_dev(k) for k in range(1, RING)]
    plane_peers = [z * PLANE + (rem + k) % PLANE for k in range(1, PLANE)]

    barrier = pltpu.get_barrier_semaphore()
    for dev in z_peers + plane_peers:
        pl.semaphore_signal(barrier, inc=1, device_id=(dev,), device_id_type=MESH)

    ld_x = pltpu.make_async_copy(img_hbm, X.at[pl.ds(0, rows)], ld_sem.at[0])
    ld_y = pltpu.make_async_copy(txt_hbm, Y.at[pl.ds(0, rows)], ld_sem.at[1])
    ld_x.start()
    ld_y.start()
    ST[...] = jnp.zeros_like(ST)

    def normalize(ref):
        blk = min(64, rows)

        def body(k, carry):
            sl = pl.ds(pl.multiple_of(k * blk, blk), blk)
            e32 = ref[sl, :].astype(F32)
            ref[sl, :] = (e32 * lax.rsqrt(jnp.sum(e32 * e32, axis=-1, keepdims=True))).astype(BF16)
            return carry

        lax.fori_loop(0, rows // blk, body, 0)

    def xrow(g, h=0):
        return g * rows + h * half

    def yrow(g, h=0, other=0):
        return g * 2 * rows + other * rows + h * half

    def remote(src, dst, ss, rs, dev):
        return pltpu.make_async_remote_copy(src_ref=src, dst_ref=dst, send_sem=ss, recv_sem=rs,
                                            device_id=(dev,), device_id_type=MESH)

    moves = [((0, 0), (1, 0), 1), ((0, 1), (1, 1), -1), ((0, 1), (2, 1), 1), ((0, 0), (2, 0), -1),
             ((1, 0), (3, 0), 1), ((1, 1), (3, 1), -1)]
    gx = []
    gy = []
    for n, (src, dst, step) in enumerate(moves):
        gx.append(remote(X.at[pl.ds(xrow(*src), half)], X.at[pl.ds(xrow(*dst), half)],
                         gx_s.at[n], gx_r.at[n], z_dev(step)))
        gy.append(remote(Y.at[pl.ds(yrow(*src), half)], Y.at[pl.ds(yrow(*dst), half)],
                         gy_s.at[n], gy_r.at[n], q_dev(step)))
    arrival = {dst: n for n, (_, dst, _) in enumerate(moves)}
    yd = {}
    for g in range(RING):
        for h in range(2):
            n = 2 * g + h
            yd[g, h] = remote(Y.at[pl.ds(yrow(g, h), half)], Y.at[pl.ds(yrow(g, h, 1), half)],
                              yd_s.at[n], yd_r.at[n], partner)

    temp2 = scal[0] * LOG2E
    bias2 = scal[1] * LOG2E

    def col_sum(val):
        return jnp.sum(val.reshape(val.shape[0] // 8, 8, val.shape[1]), axis=0)

    def logits_tile(gi, gj, other, diag):
        jrow = pl.multiple_of(gj * (2 * rows) + other * rows, rows)
        for h in range(2):
            logits_half(pl.multiple_of(gi * rows + h * half, half), jrow, h * half if diag else None)

    def logits_half(irow, jrow, shift):
        sim = dot_f32(X[pl.ds(irow, half), :], Y[pl.ds(jrow, rows), :], 1, 1)
        lg = sim * temp2 + bias2
        ex = jnp.exp2(-jnp.abs(lg))
        rc = 1.0 / (1.0 + ex)
        er = ex * rc
        wt = jnp.where(lg >= 0.0, rc, er)
        ramp = jnp.maximum(lg, 0.0)
        if shift is not None:
            same = (lax.broadcasted_iota(jnp.int32, sim.shape, 0) + shift
                    == lax.broadcasted_iota(jnp.int32, sim.shape, 1))
            wt = jnp.where(same, -jnp.where(lg >= 0.0, er, rc), wt)
            ramp = jnp.where(same, jnp.maximum(-lg, 0.0), ramp)
        H[pl.ds(irow, half), pl.ds(jrow, rows)] = wt.astype(BF16)
        ST[0] += col_sum(ramp)
        ST[1] += col_sum(wt)
        ST[2] += col_sum(wt * sim)
        prod = ex
        while prod.shape[0] > 8:
            m = prod.shape[0] // 2
            a, b = prod[:m], prod[m:]
            prod = a + b + a * b
        ST[3] += jnp.log1p(prod)

    def logits_tiles(pairs):
        def body(k, carry):
            t = k // 2
            logits_tile(pick([p[0] for p in pairs], t), pick([p[1] for p in pairs], t), k % 2, False)
            return carry

        lax.fori_loop(0, 2 * len(pairs), body, 0)

    def u_sum(dst, g, lo, hi, fresh):
        if fresh:
            dst[...] = jnp.zeros(dst.shape, F32)

        def body(k, carry):
            sl = pl.ds(pl.multiple_of(k * (2 * rows), 2 * rows), 2 * rows)
            dst[...] += dot_f32(H[pl.ds(g * rows, rows), sl], Y[sl, :], 1, 0)
            return carry

        lax.fori_loop(lo, hi, body, 0)

    def v_sum(dst, g, other, lo, hi, fresh):
        if fresh:
            dst[...] = jnp.zeros(dst.shape, F32)

        def body(k, carry):
            sl = pl.ds(pl.multiple_of(k * rows, rows), rows)
            dst[...] += dot_f32(H[sl, pl.ds(yrow(g, 0, other), rows)], X[sl, :], 0, 0)
            return carry

        lax.fori_loop(lo, hi, body, 0)

    def piece_rows(d, p):
        return pl.ds(d * half + p * piece, piece)

    def ring_copy(first, slots, s_sem, r_sem, dev, s, d, p):
        src = first if s == 0 else slots.at[s - 1]
        n = (s * 2 + d) * PIECES + p
        return remote(src.at[piece_rows(d, p)], slots.at[s, piece_rows(d, p)],
                      s_sem.at[n], r_sem.at[n], dev(1 - 2 * d))

    def u_copy(s, d, p):
        return ring_copy(PU.at[0], RU, ru_s, ru_r, z_dev, s, d, p)

    def v_copy(s, d, p):
        return ring_copy(DV.at[0], RV, rv_s, rv_r, q_dev, s, d, p)

    def serve(copy, slots, part, s, p):
        for d in range(2):
            copy(s - 1, d, p).wait_recv()
            slots[s - 1, piece_rows(d, p), :] += part[piece_rows(d, p), :]
        for d in range(2):
            copy(s, d, p).start()

    def d_copy(s):
        return remote(WV, DV.at[s % 2], dv_s.at[s], dv_r.at[s], partner)

    ld_x.wait()
    normalize(X)
    ld_y.wait()
    normalize(Y)
    pl.semaphore_wait(barrier, len(z_peers) + len(plane_peers))
    for n in range(4):
        gx[n].start()
        gy[n].start()
    for h in range(2):
        yd[0, h].start()
    logits_tile(0, 0, 0, True)
    for h in range(2):
        yd[0, h].wait_recv()
    logits_tile(0, 0, 1, False)

    def land(g):
        for h in range(2):
            n = arrival[g, h]
            gx[n].wait_recv()
            if g == 1:
                gx[n + 4].start()
            gy[n].wait_recv()
            if g == 1:
                gy[n + 4].start()
            yd[g, h].start()

    def land_other(g):
        for h in range(2):
            yd[g, h].wait_recv()

    land(1)
    land_other(1)
    logits_tiles([(0, 1), (1, 0), (1, 1)])
    u_sum(PU.at[0], 1, 0, 2, True)
    v_sum(WV, 1, 1, 0, 2, True)
    land(2)
    land_other(2)
    logits_tiles([(1, 2), (2, 1), (0, 2), (2, 0), (2, 2)])
    u_sum(PU.at[0], 1, 2, 3, False)
    v_sum(WV, 1, 1, 2, 3, False)
    land(3)
    land_other(3)
    logits_tiles([(3, 1), (1, 3)])
    v_sum(WV, 1, 1, 3, 4, False)
    d_copy(0).start()
    u_sum(PU.at[0], 1, 3, 4, False)
    for p in range(PIECES):
        for d in range(2):
            u_copy(0, d, p).start()
    logits_tiles([(0, 3)])
    d_copy(0).wait_recv()
    v_sum(DV.at[0], 1, 0, 0, 4, False)
    for p in range(PIECES):
        for d in range(2):
            v_copy(0, d, p).start()
    logits_tiles([(2, 3), (3, 0), (3, 2), (3, 3)])

    rows_out = []
    for k in range(4):
        acc = jnp.sum(ST[k], axis=0, keepdims=True)
        tot = acc[:, :128]
        for m in range(1, acc.shape[1] // 128):
            tot = tot + acc[:, m * 128:(m + 1) * 128]
        rows_out.append(tot)
    SE[0] = jnp.concatenate(rows_out + [jnp.zeros((4, 128), F32)], axis=0)
    se_z = [remote(SE.at[0], SE.at[1 + k], se_s.at[k], se_r.at[k], dev) for k, dev in enumerate(z_peers)]
    se_p = [remote(SE.at[4], SE.at[5 + k], se_s.at[3 + k], se_r.at[3 + k], dev)
            for k, dev in enumerate(plane_peers)]

    u_sum(PU.at[1], 3, 0, 4, True)
    for c in se_z:
        c.start()
    d_copy(0).wait_send()
    v_sum(WV, 3, 1, 0, 4, True)
    d_copy(1).start()
    serve(u_copy, RU, PU.at[1], 1, 0)
    d_copy(1).wait_recv()
    v_sum(DV.at[1], 3, 0, 0, 4, False)
    serve(u_copy, RU, PU.at[1], 1, 1)
    serve(v_copy, RV, DV.at[1], 1, 0)
    for c in se_z:
        c.wait_recv()
    SE[4] = SE[0] + SE[1] + SE[2] + SE[3]
    for p in range(PIECES):
        for d in range(2):
            u_copy(0, d, p).wait_send()
    u_sum(PU.at[0], 2, 0, 4, True)
    for c in se_p:
        c.start()
    serve(v_copy, RV, DV.at[1], 1, 1)
    pl.semaphore_signal(credit.at[1], inc=1, device_id=(partner,), device_id_type=MESH)
    for p in range(PIECES):
        for d in range(2):
            v_copy(0, d, p).wait_send()
    pl.semaphore_signal(credit.at[0], inc=1, device_id=(partner,), device_id_type=MESH)
    d_copy(1).wait_send()
    v_sum(WV, 2, 1, 0, 4, True)
    pl.semaphore_wait(credit.at[0], 1)
    d_copy(2).start()
    serve(u_copy, RU, PU.at[0], 2, 0)
    d_copy(2).wait_recv()
    v_sum(DV.at[0], 2, 0, 0, 4, False)
    u_sum(PU.at[1], 0, 0, 4, True)
    serve(v_copy, RV, DV.at[0], 2, 0)
    d_copy(2).wait_send()
    v_sum(WV, 0, 1, 0, 4, True)
    pl.semaphore_wait(credit.at[1], 1)
    d_copy(3).start()
    serve(u_copy, RU, PU.at[0], 2, 1)
    d_copy(3).wait_recv()
    v_sum(DV.at[1], 0, 0, 0, 4, False)
    serve(v_copy, RV, DV.at[0], 2, 1)
    for n in range(6):
        gx[n].wait_send()
        gy[n].wait_send()
    for g in range(RING):
        for h in range(2):
            yd[g, h].wait_send()
    raw_x = pltpu.make_async_copy(img_hbm, X.at[pl.ds(rows, rows)], ld_sem.at[0])
    raw_y = pltpu.make_async_copy(txt_hbm, X.at[pl.ds(2 * rows, rows)], ld_sem.at[1])
    raw_x.start()
    raw_y.start()
    for c in se_p:
        c.wait_recv()
    total = SE[4]
    for k in range(7):
        total = total + SE[5 + k]
    stat_out[...] = jnp.broadcast_to(jnp.sum(total, axis=1, keepdims=True), stat_out.shape)
    raw_x.wait()
    raw_y.wait()
    temp = scal[0]

    def finish(copy, slots, part, raw_row, out, d, p, sem):
        copy(2, d, p).wait_recv()
        blk = min(32, piece)

        def body(k, carry):
            at = d * half + p * piece + k * blk
            sl = pl.ds(pl.multiple_of(at, blk), blk)
            e32 = X[pl.ds(pl.multiple_of(raw_row + at, blk), blk), :].astype(F32)
            inv = lax.rsqrt(jnp.sum(e32 * e32, axis=-1, keepdims=True))
            unit = e32 * inv
            grad = (slots[2, sl, :] + part[sl, :]) * temp
            radial = jnp.sum(unit * grad, axis=-1, keepdims=True)
            slots[2, sl, :] = (grad - unit * radial) * inv
            return carry

        lax.fori_loop(0, piece // blk, body, 0)
        return pltpu.make_async_copy(slots.at[2, piece_rows(d, p)], out.at[piece_rows(d, p)], sem)

    outs = []
    for p in range(PIECES):
        for d in range(2):
            outs.append(finish(u_copy, RU, PU.at[1], rows, u_out, d, p, out_sem.at[len(outs)]))
            outs[-1].start()
        for d in range(2):
            outs.append(finish(v_copy, RV, DV.at[1], 2 * rows, v_out, d, p, out_sem.at[len(outs)]))
            outs[-1].start()
    for s in range(1, 3):
        for p in range(PIECES):
            for d in range(2):
                u_copy(s, d, p).wait_send()
                v_copy(s, d, p).wait_send()
    d_copy(3).wait_send()
    for c in se_z + se_p:
        c.wait_send()
    for c in outs:
        c.wait()


def solution(mesh):
    n_dev = mesh.shape['dp']

    def local_fn(img_emb, txt_emb, log_temp, logit_bias):
        rows, width = img_emb.shape
        total_rows = rows * n_dev
        temp_scale = jnp.exp(log_temp)
        scal = jnp.stack([temp_scale, logit_bias])
        dma = pltpu.SemaphoreType.DMA
        any_spec = pl.BlockSpec(memory_space=pl.ANY)
        vmem = pltpu.VMEM
        grad_img, grad_txt, stats = pl.pallas_call(
            loss_kernel,
            name='siglip_pairs',
            out_shape=(jax.ShapeDtypeStruct((rows, width), F32), jax.ShapeDtypeStruct((rows, width), F32),
                       jax.ShapeDtypeStruct((8, 128), F32)),
            in_specs=[pl.BlockSpec(memory_space=pltpu.SMEM), any_spec, any_spec],
            out_specs=(any_spec, any_spec, pl.BlockSpec(memory_space=pltpu.VMEM)),
            scratch_shapes=[
                vmem((RING * rows, width), BF16),
                vmem((2 * RING * rows, width), BF16),
                vmem((RING * rows, 2 * RING * rows), BF16),
                vmem((2, rows, width), F32),
                vmem((3, rows, width), F32),
                vmem((2, rows, width), F32),
                vmem((rows, width), F32),
                vmem((3, rows, width), F32),
                vmem((4, 8, rows), F32),
                vmem((12, 8, 128), F32),
                dma((2,)), dma((6,)), dma((6,)), dma((6,)), dma((6,)), dma((8,)), dma((8,)),
                dma((6 * PIECES,)), dma((6 * PIECES,)), dma((6 * PIECES,)), dma((6 * PIECES,)),
                dma((4,)), dma((4,)), dma((10,)), dma((10,)), dma((4 * PIECES,)),
                pltpu.SemaphoreType.REGULAR((2,)),
            ],
            compiler_params=pltpu.CompilerParams(collective_id=0, has_side_effects=True,
                                                 vmem_limit_bytes=67_000_000),
        )(scal, img_emb, txt_emb)
        sums = stats[:, 0] / total_rows
        return sums[0] * LN2 + sums[3], grad_img, grad_txt, temp_scale * sums[2], sums[1]

    return jax.shard_map(
        local_fn,
        mesh=mesh,
        in_specs=(P('dp', None), P('dp', None), P(), P()),
        out_specs=(P(), P('dp', None), P('dp', None), P(), P()),
        check_vma=False,
    )
```

time: 595 us -> 290 us (0.49)
  waiting for transfers between devices: 400 us -> 0 us
  Pallas kernels: 0 us -> 277 us
  matrix products: 116 us -> 0 us
  blocking collectives: 42.5 us -> 0 us
  other arithmetic: 17.2 us -> 1.27 us
  between operations: 17 us -> 6.19 us
    pallas_call x0 -> x1, Pallas kernels: none -> 277 us  [local_fn(): pl.pallas_call(loss_kernel, name='siglip_pairs', out_shape=(jax.ShapeDtyp...]
    reduce_scatter x2 -> x0, waiting for transfers between devices: 239 us -> none  [the longest x1 135 us: local_fn(): lax.psum_scatter(v, 'dp', scatter_dimension=0, axis_index_groups=row_grou...]
    all_gather x2 -> x0, waiting for transfers between devices: 161 us -> none  [the longest x1 96.7 us: local_fn(): lax.all_gather(img_unit.astype(jnp.bfloat16), 'dp', axis_index_groups=col...]
    dot_general x3 -> x0, matrix products: 116 us -> none  [the longest x1 57.5 us: local_fn(): sim = jnp.einsum('id,jd->ij', xs, ys, preferred_element_type=jnp.float32)]
    psum x1 -> x0, blocking collectives: 42.5 us -> none  [local_fn(): stats = lax.psum(stats, 'dp') / total_rows]
    reduce_sum x4 -> x0, other arithmetic: 6.97 us -> none  [the longest x2 4.9 us: project_back(): radial = jnp.sum(unit_rows * grad_dir, axis=-1, keepdims=True)]
  transfers between devices with their start and end apart: 4 -> 0, of which waited for: 4 -> 0; matrix products, arithmetic and copies ran while one was open for 6% -> 0% of each run, Pallas kernels for 0% -> 0%
where the time goes in v2:
time: 290 us
  Pallas kernels  277 us (96%)
  between operations  6.19 us (2%)
  local copies, waits for them, and re-layouts  5.57 us (2%)
    pallas_call x1, Pallas kernels, local_fn(): pl.pallas_call(loss_kernel, name='siglip_pairs', out_shape=(jax.ShapeDtyp...  277 us

profile of v2, /device:TPU:0, one launch (start us, length us, event | category | flops | bytes accessed | tf_op | source)
XLA Modules:
  0.0 290.0 jit_solution(7780302321341180831)
XLA Ops:
  2.0 0.6 pad_maximum_fusion.scal
  2.5 276.9 %siglip_pairs.1 = (f32[512,1280]{1,0:T(8,128)}, f32[512,1280]{1,0:T(8,128)}, f32[8,128]{1,0:T(8,128)}) custom-call(f32[2]{0:T(128)} %pad_maximum_fusion.scal, bf16[512,1280]{1,0:T(8,128)(2,1)} %img_hbm.1, bf16[512,1280]{1,0:T(8,128)(2,1)} %txt_hbm.1), custom_call_target="tpu_custom_call" | custom-call | tf_op jit(solution)/shard_map/siglip_pairs/pallas_call | solution.py:380
  279.5 0.7 slice_multiply_fusion
  280.2 0.5 fusion
  282.6 0.0 copy-start
  282.7 3.6 %copy.13 = f32[512,1280]{1,0:T(8,128)} copy(f32[512,1280]{1,0:T(8,128)} %get-tuple-element.21) | data formatting | bytes 5242880
  286.2 0.0 copy-done
  286.2 1.5 copy.14
Async XLA Ops:
  282.6 3.6 %copy-start = (f32[512,1280]{1,0:T(8,128)S(1)}, f32[512,1280]{1,0:T(8,128)}, u32[]{:S(2)}) copy-start(f32[512,1280]{1,0:T(8,128)} %get-tuple-element.22) | copy-start | bytes 7864324

commit v3 on v1

v3 whole, which is shorter than its diff:
```python
import functools
import math

import jax
import jax.numpy as jnp
from jax import lax
from jax.experimental import pallas as pl
from jax.experimental.pallas import tpu as pltpu
from jax.sharding import PartitionSpec as P

F32 = jnp.float32
BF16 = jnp.bfloat16
MESH = pl.DeviceIdType.MESH
LOG2E = math.log2(math.e)
LN2 = math.log(2.0)
PLANE = 8
SQUARE = 4
PIECES = 4


def dot_f32(lhs, rhs, lhs_dim, rhs_dim):
    return lax.dot_general(lhs, rhs, (((lhs_dim,), (rhs_dim,)), ((), ())), preferred_element_type=F32)


def pick(table, idx):
    out = jnp.int32(table[0])
    for pos in range(1, len(table)):
        out = jnp.where(idx == pos, jnp.int32(table[pos]), out)
    return out


def loss_kernel(scal, img_hbm, txt_hbm, u_out, v_out, stat_out,
                X, Y, H, PU, RU, DV, WV, RV, ST, SE,
                ld_sem, gx_s, gx_r, gy_s, gy_r, yd_s, yd_r, ru_s, ru_r, rv_s, rv_r,
                dv_s, dv_r, se_s, se_r, out_sem, credit, uz_credit, vz_credit):
    rows, width = img_hbm.shape
    half = rows // 2
    piece = rows // PIECES
    me = lax.axis_index('dp')
    z = me // PLANE
    rem = me % PLANE
    y = rem // 4
    x = (rem // 2) % 2
    core = rem % 2
    x_dev = z * PLANE + rem + 2 - 4 * x
    y_dev = z * PLANE + rem + 4 - 8 * y
    lo_dev = (z + 1 - 2 * (z % 2)) * PLANE + rem
    hi_dev = ((z + 2) % 4) * PLANE + rem
    partner = me + 1 - 2 * core
    z_peers = [((z + k) % 4) * PLANE + rem for k in range(1, 4)]
    plane_peers = [z * PLANE + (rem + k) % PLANE for k in range(1, PLANE)]

    barrier = pltpu.get_barrier_semaphore()
    for dev in z_peers + plane_peers:
        pl.semaphore_signal(barrier, inc=1, device_id=(dev,), device_id_type=MESH)

    def xrow(g, r=0):
        return g * rows + r

    def yrow(g, r=0, other=0):
        return g * 2 * rows + (r // half) * rows + other * half + r % half

    loads = []
    for h in range(2):
        loads.append(pltpu.make_async_copy(img_hbm.at[pl.ds(h * half, half)], X.at[pl.ds(h * half, half)],
                                           ld_sem.at[h]))
        loads.append(pltpu.make_async_copy(txt_hbm.at[pl.ds(h * half, half)], Y.at[pl.ds(yrow(0, h * half), half)],
                                           ld_sem.at[2 + h]))
    for c in loads:
        c.start()
    ST[...] = jnp.zeros_like(ST)

    def normalize(ref, row):
        blk = min(64, half)

        def body(k, carry):
            sl = pl.ds(pl.multiple_of(row + k * blk, blk), blk)
            e32 = ref[sl, :].astype(F32)
            ref[sl, :] = (e32 * lax.rsqrt(jnp.sum(e32 * e32, axis=-1, keepdims=True))).astype(BF16)
            return carry

        lax.fori_loop(0, half // blk, body, 0)

    def remote(src, dst, ss, rs, dev):
        return pltpu.make_async_remote_copy(src_ref=src, dst_ref=dst, send_sem=ss, recv_sem=rs,
                                            device_id=(dev,), device_id_type=MESH)

    def gather(ref, row_of, ss, rs, flat_dev, z_dev, kind, p):
        src, dst = ((0, 1), (0, 2), (2, 3))[kind]
        n = kind * PIECES + p
        return remote(ref.at[pl.ds(row_of(src, p * piece), piece)], ref.at[pl.ds(row_of(dst, p * piece), piece)],
                      ss.at[n], rs.at[n], z_dev if kind == 1 else flat_dev)

    def gx(kind, p):
        return gather(X, xrow, gx_s, gx_r, x_dev, lo_dev, kind, p)

    def gy(kind, p):
        return gather(Y, yrow, gy_s, gy_r, y_dev, hi_dev, kind, p)

    def yd(g, h):
        return remote(Y.at[pl.ds(yrow(g, h * half), half)], Y.at[pl.ds(yrow(g, h * half, 1), half)],
                      yd_s.at[2 * g + h], yd_r.at[2 * g + h], partner)

    temp2 = scal[0] * LOG2E
    bias2 = scal[1] * LOG2E

    def col_sum(val):
        return jnp.sum(val.reshape(val.shape[0] // 8, 8, val.shape[1]), axis=0)

    def logits_tile(i, j, diag=False):
        irow = pl.multiple_of(i * half, half)
        jrow = pl.multiple_of(j * rows, rows)
        sim = dot_f32(X[pl.ds(irow, half), :], Y[pl.ds(jrow, rows), :], 1, 1)
        lg = sim * temp2 + bias2
        ex = jnp.exp2(-jnp.abs(lg))
        rc = 1.0 / (1.0 + ex)
        er = ex * rc
        wt = jnp.where(lg >= 0.0, rc, er)
        ramp = jnp.maximum(lg, 0.0)
        if diag:
            same = (lax.broadcasted_iota(jnp.int32, sim.shape, 0)
                    == lax.broadcasted_iota(jnp.int32, sim.shape, 1))
            wt = jnp.where(same, -jnp.where(lg >= 0.0, er, rc), wt)
            ramp = jnp.where(same, jnp.maximum(-lg, 0.0), ramp)
        H[pl.ds(irow, half), pl.ds(jrow, rows)] = wt.astype(BF16)
        ST[0] += col_sum(ramp)
        ST[1] += col_sum(wt)
        ST[2] += col_sum(wt * sim)
        prod = ex
        while prod.shape[0] > 8:
            m = prod.shape[0] // 2
            a, b = prod[:m], prod[m:]
            prod = a + b + a * b
        ST[3] += jnp.log1p(prod)

    def logits_tiles(pairs):
        def body(k, carry):
            logits_tile(pick([p[0] for p in pairs], k), pick([p[1] for p in pairs], k))
            return carry

        lax.fori_loop(0, len(pairs), body, 0)

    def u_sum(dst, g, h_lo, h_hi):
        def body(k, carry):
            h = h_lo + k // 4
            out = pl.ds(pl.multiple_of(h * half, half), half)
            sl = pl.ds(pl.multiple_of((k % 4) * (2 * rows), 2 * rows), 2 * rows)

            @pl.when(k % 4 == 0)
            def _():
                dst[out, :] = jnp.zeros((half, width), F32)

            dst[out, :] += dot_f32(H[pl.ds(pl.multiple_of(g * rows + h * half, half), half), sl], Y[sl, :], 1, 0)
            return carry

        lax.fori_loop(0, 4 * (h_hi - h_lo), body, 0)

    def v_sum(dst, g, other, h_lo, h_hi):
        def body(k, carry):
            h = h_lo + k // 2
            out = pl.ds(pl.multiple_of(h * half, half), half)
            sl = pl.ds(pl.multiple_of((k % 2) * (2 * rows), 2 * rows), 2 * rows)
            if other:
                @pl.when(k % 2 == 0)
                def _():
                    dst[out, :] = jnp.zeros((half, width), F32)

            cols = pl.ds(pl.multiple_of(g * 2 * rows + h * rows + other * half, half), half)
            dst[out, :] += dot_f32(H[sl, cols], X[sl, :], 0, 0)
            return carry

        lax.fori_loop(0, 2 * (h_hi - h_lo), body, 0)

    def prow(p):
        return pl.ds(p * piece, piece)

    def reduce_copy(part, slots, ss, rs, flat_dev, z_dev, kind, p):
        src = (part.at[0], part.at[2], slots.at[0])[kind]
        dst = (slots.at[0], slots.at[1], part.at[1])[kind]
        n = kind * PIECES + p
        return remote(src.at[prow(p)], dst.at[prow(p)], ss.at[n], rs.at[n], z_dev if kind == 2 else flat_dev)

    def u_copy(kind, p):
        return reduce_copy(PU, RU, ru_s, ru_r, x_dev, lo_dev, kind, p)

    def v_copy(kind, p):
        return reduce_copy(DV, RV, rv_s, rv_r, y_dev, hi_dev, kind, p)

    def serve(copy, part, slots, free, z_dev, p):
        copy(0, p).wait_recv()
        slots[0, prow(p), :] += part[1, prow(p), :]
        pl.semaphore_signal(free.at[p], inc=1, device_id=(z_dev,), device_id_type=MESH)
        pl.semaphore_wait(free.at[p], 1)
        copy(2, p).start()

    def serve_u(p):
        serve(u_copy, PU, RU, uz_credit, lo_dev, p)

    def serve_v(p):
        serve(v_copy, DV, RV, vz_credit, hi_dev, p)

    slot_of = {3: 0, 2: 1, 1: 2, 0: 0}

    def d_copy(g, h):
        return remote(WV.at[pl.ds(h * half, half)], DV.at[slot_of[g], pl.ds(h * half, half)],
                      dv_s.at[2 * g + h], dv_r.at[2 * g + h], partner)

    def v_give(g, h):
        v_sum(WV, g, 1, h, h + 1)
        d_copy(g, h).start()

    def v_take(g, h):
        d_copy(g, h).wait_recv()
        v_sum(DV.at[slot_of[g]], g, 0, h, h + 1)

    def send_pair(copy, kind, h):
        for p in (2 * h, 2 * h + 1):
            copy(kind, p).start()

    for h in range(2):
        loads[2 * h].wait()
        normalize(X, h * half)
        loads[2 * h + 1].wait()
        normalize(Y, yrow(0, h * half))
    pl.semaphore_wait(barrier, len(z_peers) + len(plane_peers))
    for p in range(PIECES):
        for kind in range(2):
            gx(kind, p).start()
            gy(kind, p).start()
    for h in range(2):
        yd(0, h).start()

    def forward(p):
        gx(1, p).wait_recv()
        gx(2, p).start()
        gy(1, p).wait_recv()
        gy(2, p).start()

    def land(g, h):
        kind = g - 1
        for p in (2 * h, 2 * h + 1):
            if kind != 1:
                gx(kind, p).wait_recv()
                gy(kind, p).wait_recv()
        yd(g, h).start()

    order = [0, 1]

    def fresh(n):
        order.append(n)
        return [(n, m) for m in order[:-1]] + [(m, n) for m in order]

    for h in range(2):
        yd(0, h).wait_recv()
    logits_tile(0, 0, True)
    logits_tile(1, 1, True)
    logits_tiles([(0, 1), (1, 0)])
    land(1, 0)
    forward(0)
    yd(1, 0).wait_recv()
    logits_tiles(fresh(2))
    land(1, 1)
    forward(1)
    land(2, 0)
    yd(1, 1).wait_recv()
    yd(2, 0).wait_recv()
    logits_tiles(fresh(3) + fresh(4))
    forward(2)
    land(3, 0)
    yd(3, 0).wait_recv()
    logits_tiles(fresh(6))
    forward(3)
    land(2, 1)
    yd(2, 1).wait_recv()
    logits_tiles(fresh(5))
    land(3, 1)
    yd(3, 1).wait_recv()
    last = fresh(7)
    first = [(6, 7), (4, 7), (7, 6), (7, 4)]
    logits_tiles(first[:1])
    u_sum(PU.at[0], 3, 0, 1)
    send_pair(u_copy, 0, 0)
    logits_tiles(first[1:])
    v_give(3, 0)
    u_sum(PU.at[1], 2, 0, 1)
    v_take(3, 0)
    send_pair(v_copy, 0, 0)
    d_copy(3, 0).wait_send()
    v_give(2, 0)
    serve_u(0)
    v_take(2, 0)
    logits_tiles([t for t in last if t not in first])
    serve_v(0)
    u_sum(PU.at[0], 3, 1, 2)
    send_pair(u_copy, 0, 1)
    v_give(3, 1)
    u_sum(PU.at[1], 2, 1, 2)
    serve_u(1)
    v_take(3, 1)
    send_pair(v_copy, 0, 1)
    d_copy(3, 1).wait_send()
    v_give(2, 1)
    serve_v(1)

    rows_out = []
    for k in range(4):
        acc = jnp.sum(ST[k], axis=0, keepdims=True)
        tot = acc[:, :128]
        for m in range(1, acc.shape[1] // 128):
            tot = tot + acc[:, m * 128:(m + 1) * 128]
        rows_out.append(tot)
    SE[0] = jnp.concatenate(rows_out + [jnp.zeros((4, 128), F32)], axis=0)
    se_z = [remote(SE.at[0], SE.at[1 + k], se_s.at[k], se_r.at[k], dev) for k, dev in enumerate(z_peers)]
    se_p = [remote(SE.at[4], SE.at[5 + k], se_s.at[3 + k], se_r.at[3 + k], dev)
            for k, dev in enumerate(plane_peers)]

    v_take(2, 1)
    u_sum(PU.at[2], 1, 0, 2)
    for c in se_z:
        c.start()
    serve_u(2)
    for h in range(2):
        send_pair(u_copy, 1, h)
    for h in range(2):
        d_copy(2, h).wait_send()
        v_give(1, h)
    for h in range(2):
        v_take(1, h)
    serve_v(2)
    for h in range(2):
        send_pair(v_copy, 1, h)
    for c in se_z:
        c.wait_recv()
    SE[4] = SE[0] + SE[1] + SE[2] + SE[3]
    for h in range(2):
        d_copy(1, h).wait_send()
    v_sum(WV, 0, 1, 0, 2)
    for c in se_p:
        c.start()
    serve_u(3)
    for p in range(PIECES):
        u_copy(0, p).wait_send()
    u_sum(PU.at[0], 0, 0, 2)
    serve_v(3)
    for p in range(PIECES):
        v_copy(0, p).wait_send()
    pl.semaphore_signal(credit, inc=1, device_id=(partner,), device_id_type=MESH)
    pl.semaphore_wait(credit, 1)
    for h in range(2):
        d_copy(0, h).start()
    for h in range(2):
        v_take(0, h)
    for p in range(PIECES):
        for kind in range(3):
            gx(kind, p).wait_send()
            gy(kind, p).wait_send()
    for g in range(4):
        for h in range(2):
            yd(g, h).wait_send()
    raw_x = pltpu.make_async_copy(img_hbm, X.at[pl.ds(rows, rows)], ld_sem.at[0])
    raw_y = pltpu.make_async_copy(txt_hbm, X.at[pl.ds(2 * rows, rows)], ld_sem.at[1])
    raw_x.start()
    raw_y.start()
    for c in se_p:
        c.wait_recv()
    total = SE[4]
    for k in range(7):
        total = total + SE[5 + k]
    stat_out[...] = jnp.broadcast_to(jnp.sum(total, axis=1, keepdims=True), stat_out.shape)
    raw_x.wait()
    raw_y.wait()
    temp = scal[0]

    def finish(copy, slots, part, raw_row, out, p, sem):
        copy(1, p).wait_recv()
        copy(2, p).wait_recv()
        blk = min(32, piece)

        def body(k, carry):
            at = p * piece + k * blk
            sl = pl.ds(pl.multiple_of(at, blk), blk)
            e32 = X[pl.ds(pl.multiple_of(raw_row + at, blk), blk), :].astype(F32)
            inv = lax.rsqrt(jnp.sum(e32 * e32, axis=-1, keepdims=True))
            unit = e32 * inv
            grad = (slots[1, sl, :] + part[1, sl, :] + part[0, sl, :]) * temp
            radial = jnp.sum(unit * grad, axis=-1, keepdims=True)
            slots[1, sl, :] = (grad - unit * radial) * inv
            return carry

        lax.fori_loop(0, piece // blk, body, 0)
        return pltpu.make_async_copy(slots.at[1, prow(p)], out.at[prow(p)], sem)

    outs = []
    for p in range(PIECES):
        outs.append(finish(u_copy, RU, PU, rows, u_out, p, out_sem.at[len(outs)]))
        outs[-1].start()
        outs.append(finish(v_copy, RV, DV, 2 * rows, v_out, p, out_sem.at[len(outs)]))
        outs[-1].start()
    for p in range(PIECES):
        for kind in (1, 2):
            u_copy(kind, p).wait_send()
            v_copy(kind, p).wait_send()
    for h in range(2):
        d_copy(0, h).wait_send()
    for c in se_z + se_p:
        c.wait_send()
    for c in outs:
        c.wait()


def solution(mesh):
    n_dev = mesh.shape['dp']

    def local_fn(img_emb, txt_emb, log_temp, logit_bias):
        rows, width = img_emb.shape
        total_rows = rows * n_dev
        temp_scale = jnp.exp(log_temp)
        scal = jnp.stack([temp_scale, logit_bias])
        dma = pltpu.SemaphoreType.DMA
        any_spec = pl.BlockSpec(memory_space=pl.ANY)
        vmem = pltpu.VMEM
        grad_img, grad_txt, stats = pl.pallas_call(
            loss_kernel,
            name='siglip_pairs',
            out_shape=(jax.ShapeDtypeStruct((rows, width), F32), jax.ShapeDtypeStruct((rows, width), F32),
                       jax.ShapeDtypeStruct((8, 128), F32)),
            in_specs=[pl.BlockSpec(memory_space=pltpu.SMEM), any_spec, any_spec],
            out_specs=(any_spec, any_spec, pl.BlockSpec(memory_space=pltpu.VMEM)),
            scratch_shapes=[
                vmem((SQUARE * rows, width), BF16),
                vmem((2 * SQUARE * rows, width), BF16),
                vmem((SQUARE * rows, 2 * SQUARE * rows), BF16),
                vmem((3, rows, width), F32),
                vmem((2, rows, width), F32),
                vmem((3, rows, width), F32),
                vmem((rows, width), F32),
                vmem((2, rows, width), F32),
                vmem((4, 8, rows), F32),
                vmem((12, 8, 128), F32),
                dma((4,)), dma((3 * PIECES,)), dma((3 * PIECES,)), dma((3 * PIECES,)), dma((3 * PIECES,)),
                dma((8,)), dma((8,)),
                dma((3 * PIECES,)), dma((3 * PIECES,)), dma((3 * PIECES,)), dma((3 * PIECES,)),
                dma((8,)), dma((8,)), dma((10,)), dma((10,)), dma((2 * PIECES,)),
                pltpu.SemaphoreType.REGULAR,
                pltpu.SemaphoreType.REGULAR((PIECES,)), pltpu.SemaphoreType.REGULAR((PIECES,)),
            ],
            compiler_params=pltpu.CompilerParams(collective_id=0, has_side_effects=True,
                                                 vmem_limit_bytes=67_000_000),
        )(scal, img_emb, txt_emb)
        sums = stats[:, 0] / total_rows
        return sums[0] * LN2 + sums[3], grad_img, grad_txt, temp_scale * sums[2], sums[1]

    return jax.shard_map(
        local_fn,
        mesh=mesh,
        in_specs=(P('dp', None), P('dp', None), P(), P()),
        out_specs=(P(), P('dp', None), P('dp', None), P(), P()),
        check_vma=False,
    )
```

time: 595 us -> 243 us (0.41)
  waiting for transfers between devices: 400 us -> 0 us
  Pallas kernels: 0 us -> 230 us
  matrix products: 116 us -> 0 us
  blocking collectives: 42.5 us -> 0 us
  other arithmetic: 17.2 us -> 1.27 us
  between operations: 17 us -> 6.19 us
    reduce_scatter x2 -> x0, waiting for transfers between devices: 239 us -> none  [the longest x1 135 us: local_fn(): lax.psum_scatter(v, 'dp', scatter_dimension=0, axis_index_groups=row_grou...]
    pallas_call x0 -> x1, Pallas kernels: none -> 230 us  [local_fn(): pl.pallas_call(loss_kernel, name='siglip_pairs', out_shape=(jax.ShapeDtyp...]
    all_gather x2 -> x0, waiting for transfers between devices: 161 us -> none  [the longest x1 96.7 us: local_fn(): lax.all_gather(img_unit.astype(jnp.bfloat16), 'dp', axis_index_groups=col...]
    dot_general x3 -> x0, matrix products: 116 us -> none  [the longest x1 57.5 us: local_fn(): sim = jnp.einsum('id,jd->ij', xs, ys, preferred_element_type=jnp.float32)]
    psum x1 -> x0, blocking collectives: 42.5 us -> none  [local_fn(): stats = lax.psum(stats, 'dp') / total_rows]
    reduce_sum x4 -> x0, other arithmetic: 6.97 us -> none  [the longest x2 4.9 us: project_back(): radial = jnp.sum(unit_rows * grad_dir, axis=-1, keepdims=True)]
  transfers between devices with their start and end apart: 4 -> 0, of which waited for: 4 -> 0; matrix products, arithmetic and copies ran while one was open for 6% -> 0% of each run, Pallas kernels for 0% -> 0%
where the time goes in v3:
time: 243 us
  Pallas kernels  230 us (95%)
  between operations  6.19 us (3%)
  local copies, waits for them, and re-layouts  5.57 us (2%)
    pallas_call x1, Pallas kernels, local_fn(): pl.pallas_call(loss_kernel, name='siglip_pairs', out_shape=(jax.ShapeDtyp...  230 us
    unnamed x4, local copies, waits for them, and re-layouts  5.05 us

profile of v3, /device:TPU:0, one launch (start us, length us, event | category | flops | bytes accessed | tf_op | source)
XLA Modules:
  0.0 242.8 jit_solution(1269904639363257644)
XLA Ops:
  2.0 0.6 pad_maximum_fusion.scal
  2.5 229.8 %siglip_pairs.1 = (f32[512,1280]{1,0:T(8,128)}, f32[512,1280]{1,0:T(8,128)}, f32[8,128]{1,0:T(8,128)}) custom-call(f32[2]{0:T(128)} %pad_maximum_fusion.scal, bf16[512,1280]{1,0:T(8,128)(2,1)} %img_hbm.1, bf16[512,1280]{1,0:T(8,128)(2,1)} %txt_hbm.1), custom_call_target="tpu_custom_call" | custom-call | tf_op jit(solution)/shard_map/siglip_pairs/pallas_call | solution.py:422
  232.3 0.7 slice_multiply_fusion
  233.0 0.5 fusion
  235.5 0.0 copy-start
  235.5 3.6 %copy.13 = f32[512,1280]{1,0:T(8,128)} copy(f32[512,1280]{1,0:T(8,128)} %get-tuple-element.21) | data formatting | bytes 5242880
  239.0 0.0 copy-done
  239.0 1.5 copy.14
Async XLA Ops:
  235.5 3.6 %copy-start = (f32[512,1280]{1,0:T(8,128)S(1)}, f32[512,1280]{1,0:T(8,128)}, u32[]{:S(2)}) copy-start(f32[512,1280]{1,0:T(8,128)} %get-tuple-element.22) | copy-start | bytes 7864324

commit v4 on v3

--- a/solution.py
+++ b/solution.py
@@ -15,7 +15,7 @@
 LN2 = math.log(2.0)
 PLANE = 8
 SQUARE = 4
-PIECES = 4
+PIECES = 8
 
 
 def dot_f32(lhs, rhs, lhs_dim, rhs_dim):
@@ -213,8 +213,11 @@
         d_copy(g, h).wait_recv()
         v_sum(DV.at[slot_of[g]], g, 0, h, h + 1)
 
-    def send_pair(copy, kind, h):
-        for p in (2 * h, 2 * h + 1):
+    def pieces_of(h):
+        return range(h * PIECES // 2, (h + 1) * PIECES // 2)
+
+    def send_half(copy, kind, h):
+        for p in pieces_of(h):
             copy(kind, p).start()
 
     for h in range(2):
@@ -238,8 +241,8 @@
 
     def land(g, h):
         kind = g - 1
-        for p in (2 * h, 2 * h + 1):
-            if kind != 1:
+        if kind != 1:
+            for p in pieces_of(h):
                 gx(kind, p).wait_recv()
                 gy(kind, p).wait_recv()
         yd(g, h).start()
@@ -255,52 +258,78 @@
     logits_tile(0, 0, True)
     logits_tile(1, 1, True)
     logits_tiles([(0, 1), (1, 0)])
+    forward(0)
     land(1, 0)
-    forward(0)
+    forward(1)
     yd(1, 0).wait_recv()
     logits_tiles(fresh(2))
+    forward(2)
+    forward(3)
+    land(2, 0)
     land(1, 1)
-    forward(1)
-    land(2, 0)
+    yd(2, 0).wait_recv()
     yd(1, 1).wait_recv()
-    yd(2, 0).wait_recv()
-    logits_tiles(fresh(3) + fresh(4))
-    forward(2)
+    wave = fresh(3) + fresh(4)
+    logits_tiles(wave[:8])
+    forward(4)
+    logits_tiles(wave[8:])
+    forward(5)
     land(3, 0)
     yd(3, 0).wait_recv()
-    logits_tiles(fresh(6))
-    forward(3)
+    wave = fresh(6)
+    logits_tiles(wave[:5])
+    forward(6)
+    logits_tiles(wave[5:])
+    forward(7)
     land(2, 1)
     yd(2, 1).wait_recv()
-    logits_tiles(fresh(5))
+    rest = fresh(5)
+    now = [(5, 6), (6, 5), (5, 4), (4, 5)]
+    logits_tiles(now)
+    rest = [t for t in rest if t not in now]
     land(3, 1)
     yd(3, 1).wait_recv()
-    last = fresh(7)
-    first = [(6, 7), (4, 7), (7, 6), (7, 4)]
-    logits_tiles(first[:1])
-    u_sum(PU.at[0], 3, 0, 1)
-    send_pair(u_copy, 0, 0)
-    logits_tiles(first[1:])
+    rest += fresh(7)
+    now = [(7, 6), (6, 7), (7, 4), (4, 7)]
+    third = [(5, 2), (7, 2), (2, 5), (2, 7)]
+    rest = [t for t in rest if t not in now + third]
+    logits_tiles(now[:1])
     v_give(3, 0)
-    u_sum(PU.at[1], 2, 0, 1)
+    logits_tiles(now[1:])
     v_take(3, 0)
-    send_pair(v_copy, 0, 0)
+    send_half(v_copy, 0, 0)
     d_copy(3, 0).wait_send()
     v_give(2, 0)
+    u_sum(PU.at[0], 3, 0, 1)
+    send_half(u_copy, 0, 0)
+    v_take(2, 0)
+    serve_v(0)
+    u_sum(PU.at[1], 2, 0, 1)
     serve_u(0)
-    v_take(2, 0)
-    logits_tiles([t for t in last if t not in first])
-    serve_v(0)
+    logits_tiles(third)
+    serve_v(1)
+    serve_u(1)
+    d_copy(2, 0).wait_send()
+    v_give(1, 0)
+    u_sum(PU.at[2], 1, 0, 1)
+    send_half(u_copy, 1, 0)
+    v_take(1, 0)
+    send_half(v_copy, 1, 0)
+    serve_v(2)
+    serve_u(2)
+    logits_tiles(rest[:4])
+    serve_v(3)
+    serve_u(3)
+    logits_tiles(rest[4:])
+    v_give(3, 1)
     u_sum(PU.at[0], 3, 1, 2)
-    send_pair(u_copy, 0, 1)
-    v_give(3, 1)
-    u_sum(PU.at[1], 2, 1, 2)
-    serve_u(1)
+    send_half(u_copy, 0, 1)
     v_take(3, 1)
-    send_pair(v_copy, 0, 1)
+    send_half(v_copy, 0, 1)
     d_copy(3, 1).wait_send()
     v_give(2, 1)
-    serve_v(1)
+    u_sum(PU.at[1], 2, 1, 2)
+    v_take(2, 1)
 
     rows_out = []
     for k in range(4):
@@ -314,42 +343,46 @@
     se_p = [remote(SE.at[4], SE.at[5 + k], se_s.at[3 + k], se_r.at[3 + k], dev)
             for k, dev in enumerate(plane_peers)]
 
-    v_take(2, 1)
-    u_sum(PU.at[2], 1, 0, 2)
     for c in se_z:
         c.start()
-    serve_u(2)
-    for h in range(2):
-        send_pair(u_copy, 1, h)
-    for h in range(2):
-        d_copy(2, h).wait_send()
-        v_give(1, h)
-    for h in range(2):
-        v_take(1, h)
-    serve_v(2)
-    for h in range(2):
-        send_pair(v_copy, 1, h)
+    d_copy(2, 1).wait_send()
+    v_give(1, 1)
+    u_sum(PU.at[2], 1, 1, 2)
+    send_half(u_copy, 1, 1)
+    v_take(1, 1)
+    send_half(v_copy, 1, 1)
+    serve_v(4)
+    serve_u(4)
+    for h in range(2):
+        d_copy(1, h).wait_send()
+    v_sum(WV, 0, 1, 0, 2)
+    serve_v(5)
+    serve_u(5)
+
+    def own_room(h):
+        for p in pieces_of(h):
+            v_copy(0, p).wait_send()
+        pl.semaphore_signal(credit.at[h], inc=1, device_id=(partner,), device_id_type=MESH)
+        pl.semaphore_wait(credit.at[h], 1)
+        d_copy(0, h).start()
+        for p in pieces_of(h):
+            u_copy(0, p).wait_send()
+
+    own_room(0)
+    u_sum(PU.at[0], 0, 0, 1)
+    serve_v(6)
+    serve_u(6)
+    v_take(0, 0)
+    serve_v(7)
+    serve_u(7)
+    own_room(1)
+    u_sum(PU.at[0], 0, 1, 2)
     for c in se_z:
         c.wait_recv()
     SE[4] = SE[0] + SE[1] + SE[2] + SE[3]
-    for h in range(2):
-        d_copy(1, h).wait_send()
-    v_sum(WV, 0, 1, 0, 2)
     for c in se_p:
         c.start()
-    serve_u(3)
-    for p in range(PIECES):
-        u_copy(0, p).wait_send()
-    u_sum(PU.at[0], 0, 0, 2)
-    serve_v(3)
-    for p in range(PIECES):
-        v_copy(0, p).wait_send()
-    pl.semaphore_signal(credit, inc=1, device_id=(partner,), device_id_type=MESH)
-    pl.semaphore_wait(credit, 1)
-    for h in range(2):
-        d_copy(0, h).start()
-    for h in range(2):
-        v_take(0, h)
+    v_take(0, 1)
     for p in range(PIECES):
         for kind in range(3):
             gx(kind, p).wait_send()
@@ -361,12 +394,6 @@
     raw_y = pltpu.make_async_copy(txt_hbm, X.at[pl.ds(2 * rows, rows)], ld_sem.at[1])
     raw_x.start()
     raw_y.start()
-    for c in se_p:
-        c.wait_recv()
-    total = SE[4]
-    for k in range(7):
-        total = total + SE[5 + k]
-    stat_out[...] = jnp.broadcast_to(jnp.sum(total, axis=1, keepdims=True), stat_out.shape)
     raw_x.wait()
     raw_y.wait()
     temp = scal[0]
@@ -394,8 +421,15 @@
     for p in range(PIECES):
         outs.append(finish(u_copy, RU, PU, rows, u_out, p, out_sem.at[len(outs)]))
         outs[-1].start()
+    for p in range(PIECES):
         outs.append(finish(v_copy, RV, DV, 2 * rows, v_out, p, out_sem.at[len(outs)]))
         outs[-1].start()
+    for c in se_p:
+        c.wait_recv()
+    total = SE[4]
+    for k in range(7):
+        total = total + SE[5 + k]
+    stat_out[...] = jnp.broadcast_to(jnp.sum(total, axis=1, keepdims=True), stat_out.shape)
     for p in range(PIECES):
         for kind in (1, 2):
             u_copy(kind, p).wait_send()
@@ -441,7 +475,7 @@
                 dma((8,)), dma((8,)),
                 dma((3 * PIECES,)), dma((3 * PIECES,)), dma((3 * PIECES,)), dma((3 * PIECES,)),
                 dma((8,)), dma((8,)), dma((10,)), dma((10,)), dma((2 * PIECES,)),
-                pltpu.SemaphoreType.REGULAR,
+                pltpu.SemaphoreType.REGULAR((2,)),
                 pltpu.SemaphoreType.REGULAR((PIECES,)), pltpu.SemaphoreType.REGULAR((PIECES,)),
             ],
             compiler_params=pltpu.CompilerParams(collective_id=0, has_side_effects=True,

time: 243 us -> 230 us (0.947)
  Pallas kernels: 230 us -> 217 us
    pallas_call x1, Pallas kernels: 230 us -> 217 us  [local_fn(): pl.pallas_call(loss_kernel, name='siglip_pairs', out_shape=(jax.ShapeDtyp...]
where the time goes in v4:
time: 230 us
  Pallas kernels  217 us (94%)
  between operations  6.19 us (3%)
  local copies, waits for them, and re-layouts  5.57 us (2%)
    pallas_call x1, Pallas kernels, local_fn(): pl.pallas_call(loss_kernel, name='siglip_pairs', out_shape=(jax.ShapeDtyp...  217 us
    unnamed x4, local copies, waits for them, and re-layouts  5.05 us

profile of v4, /device:TPU:0, one launch (start us, length us, event | category | flops | bytes accessed | tf_op | source)
XLA Modules:
  0.0 230.0 jit_solution(11048429076121117317)
XLA Ops:
  2.0 0.6 pad_maximum_fusion.scal
  2.5 217.0 %siglip_pairs.1 = (f32[512,1280]{1,0:T(8,128)}, f32[512,1280]{1,0:T(8,128)}, f32[8,128]{1,0:T(8,128)}) custom-call(f32[2]{0:T(128)} %pad_maximum_fusion.scal, bf16[512,1280]{1,0:T(8,128)(2,1)} %img_hbm.1, bf16[512,1280]{1,0:T(8,128)(2,1)} %txt_hbm.1), custom_call_target="tpu_custom_call" | custom-call | tf_op jit(solution)/shard_map/siglip_pairs/pallas_call | solution.py:456
  219.5 0.7 slice_multiply_fusion
  220.2 0.5 fusion
  222.7 0.0 copy-start
  222.7 3.6 %copy.13 = f32[512,1280]{1,0:T(8,128)} copy(f32[512,1280]{1,0:T(8,128)} %get-tuple-element.21) | data formatting | bytes 5242880
  226.3 0.0 copy-done
  226.3 1.5 copy.14
Async XLA Ops:
  222.7 3.6 %copy-start = (f32[512,1280]{1,0:T(8,128)S(1)}, f32[512,1280]{1,0:T(8,128)}, u32[]{:S(2)}) copy-start(f32[512,1280]{1,0:T(8,128)} %get-tuple-element.22) | copy-start | bytes 7864324

commit v5 on v4

--- a/solution.py
+++ b/solution.py
@@ -29,7 +29,7 @@
     return out
 
 
-def loss_kernel(scal, img_hbm, txt_hbm, u_out, v_out, stat_out,
+def loss_kernel(log_temp, logit_bias, img_hbm, txt_hbm, u_out, v_out, stat_out,
                 X, Y, H, PU, RU, DV, WV, RV, ST, SE,
                 ld_sem, gx_s, gx_r, gy_s, gy_r, yd_s, yd_r, ru_s, ru_r, rv_s, rv_r,
                 dv_s, dv_r, se_s, se_r, out_sem, credit, uz_credit, vz_credit):
@@ -97,12 +97,20 @@
     def gy(kind, p):
         return gather(Y, yrow, gy_s, gy_r, y_dev, hi_dev, kind, p)
 
-    def yd(g, h):
-        return remote(Y.at[pl.ds(yrow(g, h * half), half)], Y.at[pl.ds(yrow(g, h * half, 1), half)],
-                      yd_s.at[2 * g + h], yd_r.at[2 * g + h], partner)
-
-    temp2 = scal[0] * LOG2E
-    bias2 = scal[1] * LOG2E
+    def yd(g, p):
+        return remote(Y.at[pl.ds(yrow(g, p * piece), piece)], Y.at[pl.ds(yrow(g, p * piece, 1), piece)],
+                      yd_s.at[g * PIECES + p], yd_r.at[g * PIECES + p], partner)
+
+    def pieces_of(h):
+        return range(h * PIECES // 2, (h + 1) * PIECES // 2)
+
+    def other_core(g, h):
+        for p in pieces_of(h):
+            yd(g, p).wait_recv()
+
+    temp = jnp.max(jnp.exp(jnp.full((8, 128), log_temp[0], F32)))
+    temp2 = temp * LOG2E
+    bias2 = logit_bias[0] * LOG2E
 
     def col_sum(val):
         return jnp.sum(val.reshape(val.shape[0] // 8, 8, val.shape[1]), axis=0)
@@ -133,12 +141,14 @@
             prod = a + b + a * b
         ST[3] += jnp.log1p(prod)
 
-    def logits_tiles(pairs):
+    def logits_tiles(pairs, per_step=2):
         def body(k, carry):
-            logits_tile(pick([p[0] for p in pairs], k), pick([p[1] for p in pairs], k))
+            for n in range(per_step):
+                part = pairs[n::per_step]
+                logits_tile(pick([p[0] for p in part], k), pick([p[1] for p in part], k))
             return carry
 
-        lax.fori_loop(0, len(pairs), body, 0)
+        lax.fori_loop(0, len(pairs) // per_step, body, 0)
 
     def u_sum(dst, g, h_lo, h_hi):
         def body(k, carry):
@@ -205,6 +215,21 @@
         return remote(WV.at[pl.ds(h * half, half)], DV.at[slot_of[g], pl.ds(h * half, half)],
                       dv_s.at[2 * g + h], dv_r.at[2 * g + h], partner)
 
+    quarter = half // 2
+
+    def first_copy(n):
+        sl = pl.ds(n * quarter, quarter)
+        return remote(WV.at[sl], DV.at[0, sl], dv_s.at[8 + n], dv_r.at[8 + n], partner)
+
+    def first_sum(dst, n, other):
+        out = pl.ds(n * quarter, quarter)
+        cols = pl.ds(yrow(3, n * quarter, other), quarter)
+        val = dot_f32(H[:, cols], X[...], 0, 0)
+        if other:
+            dst[out, :] = val
+        else:
+            dst[out, :] += val
+
     def v_give(g, h):
         v_sum(WV, g, 1, h, h + 1)
         d_copy(g, h).start()
@@ -212,9 +237,6 @@
     def v_take(g, h):
         d_copy(g, h).wait_recv()
         v_sum(DV.at[slot_of[g]], g, 0, h, h + 1)
-
-    def pieces_of(h):
-        return range(h * PIECES // 2, (h + 1) * PIECES // 2)
 
     def send_half(copy, kind, h):
         for p in pieces_of(h):
@@ -230,22 +252,22 @@
         for kind in range(2):
             gx(kind, p).start()
             gy(kind, p).start()
-    for h in range(2):
-        yd(0, h).start()
+    for p in range(PIECES):
+        yd(0, p).start()
 
     def forward(p):
+        gy(1, p).wait_recv()
+        gy(2, p).start()
+        yd(2, p).start()
         gx(1, p).wait_recv()
         gx(2, p).start()
-        gy(1, p).wait_recv()
-        gy(2, p).start()
 
     def land(g, h):
-        kind = g - 1
-        if kind != 1:
-            for p in pieces_of(h):
-                gx(kind, p).wait_recv()
-                gy(kind, p).wait_recv()
-        yd(g, h).start()
+        for p in pieces_of(h):
+            gy(g - 1, p).wait_recv()
+            yd(g, p).start()
+        for p in pieces_of(h):
+            gx(g - 1, p).wait_recv()
 
     order = [0, 1]
 
@@ -254,67 +276,73 @@
         return [(n, m) for m in order[:-1]] + [(m, n) for m in order]
 
     for h in range(2):
-        yd(0, h).wait_recv()
+        other_core(0, h)
     logits_tile(0, 0, True)
     logits_tile(1, 1, True)
-    logits_tiles([(0, 1), (1, 0)])
+    logits_tiles([(0, 1), (1, 0)], 1)
     forward(0)
     land(1, 0)
     forward(1)
-    yd(1, 0).wait_recv()
-    logits_tiles(fresh(2))
+    other_core(1, 0)
+    wave = fresh(2)
+    logits_tiles(wave[:4], 1)
+    wave = wave[4:]
     forward(2)
     forward(3)
-    land(2, 0)
     land(1, 1)
-    yd(2, 0).wait_recv()
-    yd(1, 1).wait_recv()
-    wave = fresh(3) + fresh(4)
-    logits_tiles(wave[:8])
+    other_core(2, 0)
+    other_core(1, 1)
+    wave += fresh(3) + fresh(4)
+    logits_tiles(wave[:8], 1)
     forward(4)
-    logits_tiles(wave[8:])
+    logits_tiles(wave[8:16], 1)
     forward(5)
     land(3, 0)
-    yd(3, 0).wait_recv()
-    wave = fresh(6)
-    logits_tiles(wave[:5])
+    other_core(3, 0)
+    wave = wave[16:] + fresh(6)
+    logits_tiles(wave[:6])
     forward(6)
-    logits_tiles(wave[5:])
+    logits_tiles(wave[6:])
     forward(7)
-    land(2, 1)
-    yd(2, 1).wait_recv()
+    other_core(2, 1)
     rest = fresh(5)
     now = [(5, 6), (6, 5), (5, 4), (4, 5)]
     logits_tiles(now)
     rest = [t for t in rest if t not in now]
     land(3, 1)
-    yd(3, 1).wait_recv()
+    other_core(3, 1)
     rest += fresh(7)
     now = [(7, 6), (6, 7), (7, 4), (4, 7)]
     third = [(5, 2), (7, 2), (2, 5), (2, 7)]
     rest = [t for t in rest if t not in now + third]
-    logits_tiles(now[:1])
-    v_give(3, 0)
-    logits_tiles(now[1:])
-    v_take(3, 0)
-    send_half(v_copy, 0, 0)
-    d_copy(3, 0).wait_send()
-    v_give(2, 0)
+    logits_tiles(now[:2])
+    for n in range(2):
+        first_sum(WV, n, 1)
+        first_copy(n).start()
+    for n in range(2):
+        first_copy(n).wait_recv()
+        first_sum(DV.at[0], n, 0)
+        for p in range(n * PIECES // 4, (n + 1) * PIECES // 4):
+            v_copy(0, p).start()
     u_sum(PU.at[0], 3, 0, 1)
     send_half(u_copy, 0, 0)
+    logits_tiles(now[2:])
+    for n in range(2):
+        first_copy(n).wait_send()
+    v_give(2, 0)
     v_take(2, 0)
     serve_v(0)
     u_sum(PU.at[1], 2, 0, 1)
     serve_u(0)
     logits_tiles(third)
-    serve_v(1)
-    serve_u(1)
     d_copy(2, 0).wait_send()
     v_give(1, 0)
+    serve_v(1)
+    v_take(1, 0)
+    send_half(v_copy, 1, 0)
+    serve_u(1)
     u_sum(PU.at[2], 1, 0, 1)
     send_half(u_copy, 1, 0)
-    v_take(1, 0)
-    send_half(v_copy, 1, 0)
     serve_v(2)
     serve_u(2)
     logits_tiles(rest[:4])
@@ -347,11 +375,11 @@
         c.start()
     d_copy(2, 1).wait_send()
     v_give(1, 1)
+    serve_v(4)
+    v_take(1, 1)
+    send_half(v_copy, 1, 1)
     u_sum(PU.at[2], 1, 1, 2)
     send_half(u_copy, 1, 1)
-    v_take(1, 1)
-    send_half(v_copy, 1, 1)
-    serve_v(4)
     serve_u(4)
     for h in range(2):
         d_copy(1, h).wait_send()
@@ -388,15 +416,14 @@
             gx(kind, p).wait_send()
             gy(kind, p).wait_send()
     for g in range(4):
-        for h in range(2):
-            yd(g, h).wait_send()
+        for p in range(PIECES):
+            yd(g, p).wait_send()
     raw_x = pltpu.make_async_copy(img_hbm, X.at[pl.ds(rows, rows)], ld_sem.at[0])
     raw_y = pltpu.make_async_copy(txt_hbm, X.at[pl.ds(2 * rows, rows)], ld_sem.at[1])
     raw_x.start()
     raw_y.start()
     raw_x.wait()
     raw_y.wait()
-    temp = scal[0]
 
     def finish(copy, slots, part, raw_row, out, p, sem):
         copy(1, p).wait_recv()
@@ -449,7 +476,6 @@
         rows, width = img_emb.shape
         total_rows = rows * n_dev
         temp_scale = jnp.exp(log_temp)
-        scal = jnp.stack([temp_scale, logit_bias])
         dma = pltpu.SemaphoreType.DMA
         any_spec = pl.BlockSpec(memory_space=pl.ANY)
         vmem = pltpu.VMEM
@@ -458,7 +484,7 @@
             name='siglip_pairs',
             out_shape=(jax.ShapeDtypeStruct((rows, width), F32), jax.ShapeDtypeStruct((rows, width), F32),
                        jax.ShapeDtypeStruct((8, 128), F32)),
-            in_specs=[pl.BlockSpec(memory_space=pltpu.SMEM), any_spec, any_spec],
+            in_specs=[pl.BlockSpec(memory_space=pltpu.SMEM)] * 2 + [any_spec] * 2,
             out_specs=(any_spec, any_spec, pl.BlockSpec(memory_space=pltpu.VMEM)),
             scratch_shapes=[
                 vmem((SQUARE * rows, width), BF16),
@@ -472,15 +498,15 @@
                 vmem((4, 8, rows), F32),
                 vmem((12, 8, 128), F32),
                 dma((4,)), dma((3 * PIECES,)), dma((3 * PIECES,)), dma((3 * PIECES,)), dma((3 * PIECES,)),
-                dma((8,)), dma((8,)),
+                dma((4 * PIECES,)), dma((4 * PIECES,)),
                 dma((3 * PIECES,)), dma((3 * PIECES,)), dma((3 * PIECES,)), dma((3 * PIECES,)),
-                dma((8,)), dma((8,)), dma((10,)), dma((10,)), dma((2 * PIECES,)),
+                dma((10,)), dma((10,)), dma((10,)), dma((10,)), dma((2 * PIECES,)),
                 pltpu.SemaphoreType.REGULAR((2,)),
                 pltpu.SemaphoreType.REGULAR((PIECES,)), pltpu.SemaphoreType.REGULAR((PIECES,)),
             ],
             compiler_params=pltpu.CompilerParams(collective_id=0, has_side_effects=True,
                                                  vmem_limit_bytes=67_000_000),
-        )(scal, img_emb, txt_emb)
+        )(log_temp.reshape(1), logit_bias.reshape(1), img_emb, txt_emb)
         sums = stats[:, 0] / total_rows
         return sums[0] * LN2 + sums[3], grad_img, grad_txt, temp_scale * sums[2], sums[1]
 

time: 230 us -> 226 us (0.983)
  Pallas kernels: 217 us -> 212 us
    pallas_call x1, Pallas kernels: 217 us -> 212 us  [local_fn(): pl.pallas_call(loss_kernel, name='siglip_pairs', out_shape=(jax.ShapeDtyp...]
where the time goes in v5:
time: 226 us; the launch traced here: 225 us
  Pallas kernels  212 us (94%)
  between operations  6.19 us (3%)
  local copies, waits for them, and re-layouts  5.57 us (2%)
    pallas_call x1, Pallas kernels, local_fn(): pl.pallas_call(loss_kernel, name='siglip_pairs', out_shape=(jax.ShapeDtyp...  212 us
    unnamed x4, local copies, waits for them, and re-layouts  5.05 us

profile of v5, /device:TPU:0, one launch (start us, length us, event | category | flops | bytes accessed | tf_op | source)
XLA Modules:
  0.0 224.5 jit_solution(5780322923353182161)
XLA Ops:
  2.0 212.1 %siglip_pairs.1 = (f32[512,1280]{1,0:T(8,128)}, f32[512,1280]{1,0:T(8,128)}, f32[8,128]{1,0:T(8,128)}) custom-call(f32[1]{0:T(128)} %bitcast.5.log_temp, f32[1]{0:T(128)} %bitcast.6.logit_bias, bf16[512,1280]{1,0:T(8,128)(2,1)} %img_hbm.1, bf16[512,1280]{1,0:T(8,128)(2,1)} %txt_hbm.1), custom_call_target="tpu_custom_call" | custom-call | tf_op jit(solution)/shard_map/siglip_pairs/pallas_call | solution.py:482
  214.0 0.7 slice_multiply_fusion
  214.7 0.5 fusion
  217.2 0.0 copy-start
  217.2 3.6 %copy.13 = f32[512,1280]{1,0:T(8,128)} copy(f32[512,1280]{1,0:T(8,128)} %get-tuple-element.21) | data formatting | bytes 5242880
  220.7 0.0 copy-done
  220.7 1.5 copy.14
Async XLA Ops:
  217.2 3.6 %copy-start = (f32[512,1280]{1,0:T(8,128)S(1)}, f32[512,1280]{1,0:T(8,128)}, u32[]{:S(2)}) copy-start(f32[512,1280]{1,0:T(8,128)} %get-tuple-element.22) | copy-start | bytes 7864324
